TPU v7x, 32 devices: a whole 2x2x4 slice. The times are simulated.
32 devices in a mesh: seq: 4 (over z), tp: 8 (over y, x, core).
Axes of the slice: x: 2, y: 2, z: 4, core: 2. Of those that a mesh axis runs over, the one named last changes fastest.
Arguments:
- tokens: bfloat16 [2048, 4096], P('seq'), may hold values from -80 to 80
- norm_gain: float32 [4096], replicated, may hold values from 0.1 to 1.9
- query_weight: bfloat16 [4096, 4096], P(None, 'tp'), may hold values from -1 to 1
- key_weight: bfloat16 [4096, 1024], P(None, 'tp'), may hold values from -8 to 8
- value_weight: bfloat16 [4096, 1024], P(None, 'tp'), may hold values from -0.09375 to 0.09375
- out_weight: bfloat16 [4096, 4096], P(None, 'tp'), may hold values from -1 to 1
- segments: int32 [2048], replicated, may hold values from 0 to 2, never falling along the last dimension, each value on 1 to 1024 neighbouring positions
Outputs:
- attn_out: bfloat16 [2048, 4096], P('seq', 'tp')
All inputs are finite; a program needn't handle non-finite values.
Results may differ from a plain program's by a relative error of at most 0.013.
The roundings to bfloat16 on the way count: a program that leaves them out, or rounds other values in their place, can miss the bound.
Values may be sent and summed in bfloat16 or wider, within the bound.
No kernel may reach another device: no remote copies, remote signals or barrier semaphores. Data moves between devices by JAX's collectives and lax.ppermute only.
A program may use at most 128 MiB of HBM per device.

v0:
```python
import functools
import math

import jax
import jax.numpy as jnp
import numpy as np
from jax import lax
from jax.experimental import pallas as pl
from jax.experimental.pallas import tpu as pltpu
from jax.sharding import PartitionSpec as P

HEAD_DIM = 128
WINDOW = 4096
EPSILON = 1e-05
BASE = 10000.0


VMEM = pl.BlockSpec(memory_space=pltpu.VMEM)
HBM = pl.BlockSpec(memory_space=pltpu.HBM)
PARAMS = pltpu.CompilerParams(vmem_limit_bytes=16 << 20)


def in_hbm(*arrays):
    return [pltpu.with_memory_space_constraint(a, pltpu.HBM) for a in arrays]


def rotation_tables(block_rows, blocks):
    freqs = BASE ** (-2.0 * (np.arange(HEAD_DIM) % (HEAD_DIM // 2)) / HEAD_DIM)
    row = np.arange(block_rows)[:, None] * freqs
    start = (np.arange(blocks) * block_rows)[:, None] * freqs
    tables = (np.cos(row), np.sin(row), np.cos(start), np.sin(start))
    return [jnp.asarray(t, jnp.float32) for t in tables]


def rotate(x, cosine, sine):
    return (x * cosine + pltpu.roll(x, HEAD_DIM // 2, 1) * sine).astype(jnp.bfloat16)


def heads_of(width):
    return [slice(h, h + HEAD_DIM) for h in range(0, width, HEAD_DIM)]


def normalise(tokens, gain):
    wide = tokens.astype(jnp.float32)
    scale = lax.rsqrt(jnp.mean(wide * wide, axis=-1, keepdims=True) + EPSILON)
    return (wide * scale * gain).astype(jnp.bfloat16)


def key_value_of(normed, weight, cosine, sine, kv_ref, here):
    product = jnp.dot(normed, weight, preferred_element_type=jnp.float32)
    width = kv_ref.shape[1] // 2
    for h in heads_of(width):
        kv_ref[here, h] = rotate(product[:, h], cosine, sine)
    kv_ref[here, width:] = product[:, width:].astype(jnp.bfloat16)


def second_half_kernel(
    tile, tokens, gain, key_weight, value_weight, row_cos, row_sin, start_cos, start_sin,
    kv_ref, normed_ref, weight, first_tokens, gain_copy, cosine, sine,
    held, row_c, row_s, start_c, start_s, tile_sems, sems,
):
    rows, width = kv_ref.shape[0], key_weight.shape[1]
    steps = rows // tile
    tiles = [
        pltpu.make_async_copy(
            tokens.at[rows + i * tile : rows + (i + 1) * tile, :],
            held.at[i * tile : (i + 1) * tile, :],
            tile_sems.at[i],
        )
        for i in range(steps)
    ]
    moves = [
        (gain, gain_copy),
        (key_weight, weight.at[:, :width]),
        (value_weight, weight.at[:, width:]),
        (row_cos, row_c),
        (row_sin, row_s),
        (start_cos, start_c),
        (start_sin, start_s),
        (tokens.at[:rows, :], first_tokens),
    ]
    moves = [pltpu.make_async_copy(a, b, sems.at[i]) for i, (a, b) in enumerate(moves)]
    tiles[0].start()
    moves[0].start()
    for move in moves[1:3]:
        move.start()
    for copy in tiles[1:]:
        copy.start()
    for move in moves[3:]:
        move.start()
    moves[0].wait()
    for i in range(steps):
        here = slice(i * tile, (i + 1) * tile)
        tiles[i].wait()
        normed_ref[here, :] = normalise(held[here, :], gain_copy[...])
    for move in moves[3:7]:
        move.wait()
    block = lax.axis_index("seq")
    cos_b, sin_b = start_c[pl.ds(block, 1), :], start_s[pl.ds(block, 1), :]
    cos_r, sin_r = row_c[...], row_s[...]
    lane = lax.broadcasted_iota(jnp.int32, cos_r.shape, 1)
    cosine[...] = cos_r * cos_b - sin_r * sin_b
    turned = sin_r * cos_b + cos_r * sin_b
    sine[...] = jnp.where(lane < HEAD_DIM // 2, -turned, turned)
    moves[1].wait()
    moves[2].wait()
    key_value_of(normed_ref[...], weight[...], cosine[rows:, :], sine[rows:, :], kv_ref, slice(None))
    moves[7].wait()


def second_half(tokens, gain, key_weight, value_weight, tables):
    block_rows, depth = tokens.shape
    half, width = block_rows // 2, key_weight.shape[1]
    tile = min(half, 64)
    shape, bf16, f32 = jax.ShapeDtypeStruct, jnp.bfloat16, jnp.float32
    return pl.pallas_call(
        functools.partial(second_half_kernel, tile),
        out_shape=(
            shape((half, 2 * width), bf16),
            shape((half, depth), bf16),
            shape((depth, 2 * width), bf16),
            shape((half, depth), bf16),
            shape(gain.shape, f32),
            shape((block_rows, HEAD_DIM), f32),
            shape((block_rows, HEAD_DIM), f32),
        ),
        in_specs=[HBM] * 8,
        out_specs=(VMEM,) * 7,
        scratch_shapes=[pltpu.VMEM((half, depth), bf16)]
        + [pltpu.VMEM(t.shape, f32) for t in tables]
        + [pltpu.SemaphoreType.DMA((half // tile,)), pltpu.SemaphoreType.DMA((8,))],
        compiler_params=PARAMS,
        name="second_half",
    )(*in_hbm(tokens, gain, key_weight, value_weight, *tables))


def first_half_kernel(tokens, gain, weight, cosine, sine, query_weight, kv_ref, normed_ref, query_copy, sem):
    move = pltpu.make_async_copy(query_weight, query_copy, sem)
    move.start()
    rows = kv_ref.shape[0]
    normed_ref[...] = normalise(tokens[...], gain[...])
    key_value_of(normed_ref[...], weight[...], cosine[:rows, :], sine[:rows, :], kv_ref, slice(None))
    move.wait()


def first_half(tokens, gain, weight, cosine, sine, query_weight):
    half = tokens.shape[0]
    return pl.pallas_call(
        first_half_kernel,
        out_shape=(
            jax.ShapeDtypeStruct((half, weight.shape[1]), jnp.bfloat16),
            jax.ShapeDtypeStruct(tokens.shape, jnp.bfloat16),
            jax.ShapeDtypeStruct(query_weight.shape, jnp.bfloat16),
        ),
        in_specs=[VMEM] * 5 + [HBM],
        out_specs=(VMEM,) * 3,
        scratch_shapes=[pltpu.SemaphoreType.DMA],
        compiler_params=PARAMS,
        name="first_half",
    )(tokens, gain, weight, cosine, sine, *in_hbm(query_weight))


def query_kernel(part, normed, weight, cosine, sine, out_ref):
    rows = slice(part * normed.shape[0], (part + 1) * normed.shape[0])
    product = jnp.dot(normed[...], weight[...], preferred_element_type=jnp.float32)
    for h in heads_of(weight.shape[1]):
        out_ref[:, h] = rotate(product[:, h], cosine[rows, :], sine[rows, :])


def query(part, normed, weight, cosine, sine):
    return pl.pallas_call(
        functools.partial(query_kernel, part),
        out_shape=jax.ShapeDtypeStruct((normed.shape[0], weight.shape[1]), jnp.bfloat16),
        in_specs=[VMEM] * 4,
        out_specs=VMEM,
        compiler_params=PARAMS,
    )(normed, weight, cosine, sine)


def attend_kernel(part, back, limits, q_ref, *refs):
    kv_refs, out_ref, bias_ref = refs[:-2], refs[-2], refs[-1]
    rows, half = q_ref.shape[0], kv_refs[0].shape[0]
    kv_width = kv_refs[0].shape[1] // 2
    group = q_ref.shape[1] // kv_width
    factor = math.log2(math.e) / math.sqrt(HEAD_DIM)
    places = [slice(p * half, (p + 1) * half) for p in range(back + 1)]
    base = (2 * lax.axis_index("seq") + part) * half
    row = base + lax.broadcasted_iota(jnp.int32, (rows, HEAD_DIM), 0)
    start = jnp.where(row >= limits[1], limits[1], jnp.where(row >= limits[0], limits[0], 0))
    start = jnp.maximum(start, row - (WINDOW - 1))
    for place, span in enumerate(places):
        first = base - (back - place) * half
        for left in range(0, half, HEAD_DIM):
            key = first + left + lax.broadcasted_iota(jnp.int32, (rows, HEAD_DIM), 1)
            mask = key >= start
            if place == back:
                mask = mask & (key <= row)
            bias_ref[:, place * half + left : place * half + left + HEAD_DIM] = jnp.where(
                mask, jnp.float32(0), jnp.float32(-1e30)
            )
    ones = jnp.ones((half, HEAD_DIM), jnp.bfloat16)
    for h, head in enumerate(heads_of(q_ref.shape[1])):
        first = (h // group) * HEAD_DIM
        keys, vals = slice(first, first + HEAD_DIM), slice(kv_width + first, kv_width + first + HEAD_DIM)
        q = q_ref[:, head]
        scores = [
            lax.dot_general(q, kv[:, keys], (((1,), (1,)), ((), ())), preferred_element_type=jnp.float32)
            * factor
            + bias_ref[:, span]
            for kv, span in zip(kv_refs, places)
        ]
        peak = jnp.max(functools.reduce(jnp.maximum, scores), axis=-1, keepdims=True)
        summed = 0.0
        for s, kv in zip(scores, kv_refs):
            w = jnp.exp2(s - peak).astype(jnp.bfloat16)
            both = jnp.concatenate([kv[:, vals], ones], axis=1)
            summed = summed + jnp.dot(w, both, preferred_element_type=jnp.float32)
        out_ref[:, head] = (summed[:, :HEAD_DIM] / summed[:, HEAD_DIM:]).astype(jnp.bfloat16)


def attend(part, queries, limits, key_values):
    half = queries.shape[0]
    back = len(key_values) - 1
    return pl.pallas_call(
        functools.partial(attend_kernel, part, back),
        out_shape=jax.ShapeDtypeStruct(queries.shape, jnp.bfloat16),
        in_specs=[pl.BlockSpec(memory_space=pltpu.SMEM)] + [VMEM] * (1 + len(key_values)),
        out_specs=VMEM,
        scratch_shapes=[pltpu.VMEM((half, (back + 1) * half), jnp.float32)],
        compiler_params=PARAMS,
    )(limits, queries, *key_values)


def added(bits, total, weight, xs):
    depth = xs[0].shape[1]
    me = lax.axis_index("tp")
    for bit, x in zip(bits, xs):
        owner = jnp.bitwise_xor(me, bit)
        rows = pl.ds(pl.multiple_of(owner * depth, depth), depth)
        total = total + jnp.dot(x[...], weight[rows, :], preferred_element_type=jnp.float32)
    return total


def product_kernel(bits, extra, weight, *refs):
    xs, out_ref = refs[: len(bits)], refs[-1]
    out_ref[...] = added(bits, refs[len(bits)][...] if extra else 0.0, weight, xs)


def product(weight, got, total=None):
    bits, xs = zip(*got)
    extra = () if total is None else (total,)
    return pl.pallas_call(
        functools.partial(product_kernel, bits, bool(extra)),
        out_shape=jax.ShapeDtypeStruct((xs[0].shape[0], weight.shape[1]), jnp.float32),
        in_specs=[VMEM] * (1 + len(xs) + len(extra)),
        out_specs=VMEM,
        compiler_params=PARAMS,
    )(weight, *xs, *extra)


def store_kernel(part, bits, weight, *refs):
    xs, total = refs[: len(bits)], refs[len(bits)]
    out_ref, rounded, sem = refs[-3:]
    rounded[...] = added(bits, total[...], weight, xs).astype(rounded.dtype)
    half = rounded.shape[0]
    move = pltpu.make_async_copy(rounded, out_ref.at[part * half : (part + 1) * half, :], sem)
    move.start()
    move.wait()


def store(part, weight, got, total, out=None):
    bits, xs = zip(*got)
    half, width = total.shape
    extra = () if out is None else in_hbm(out)
    count = 2 + len(xs)
    return pl.pallas_call(
        functools.partial(store_kernel, part, bits),
        out_shape=pltpu.HBM((2 * half, width), jnp.bfloat16),
        in_specs=[VMEM] * count + [HBM] * len(extra),
        out_specs=HBM,
        scratch_shapes=[pltpu.VMEM((half, width), jnp.bfloat16), pltpu.SemaphoreType.DMA],
        input_output_aliases={count: 0} if extra else {},
        compiler_params=PARAMS,
    )(weight, *xs, total, *extra)


def shards(tokens, norm_gain, query_weight, key_weight, value_weight, out_weight, segments):
    block_rows = tokens.shape[0]
    half = block_rows // 2
    seq_count, tp_count = lax.axis_size("seq"), lax.axis_size("tp")
    total = block_rows * seq_count
    reach = min(WINDOW, total // 2)
    back = min((reach - 2) // half + 1, 2 * seq_count - 1)
    ring = [(i, (i + 1) % seq_count) for i in range(seq_count)]
    limits = jnp.sum((segments[None, :] < jnp.array([[1], [2]], jnp.int32)).astype(jnp.int32), axis=1)

    halves, normed, queries = [None] * (back + 2), [None, None], [None, None]
    halves[0], normed[1], weight, first_tokens, gain, cosine, sine = second_half(
        tokens, norm_gain[None, :], key_weight, value_weight, rotation_tables(block_rows, seq_count)
    )
    halves[1], normed[0], query_copy = first_half(first_tokens, gain, weight, cosine, sine, query_weight)
    for distance in range(2, back + 2):
        halves[distance] = lax.ppermute(halves[distance - 2], "seq", ring)
    for part in (1, 0):
        queries[part] = query(part, normed[part], query_copy, cosine, sine)

    def swap(x, bit):
        return lax.ppermute(x, "tp", [(i, i ^ bit) for i in range(tp_count)])

    got, out = {}, None
    for part in (1, 0):
        mine = attend(part, queries[part], limits, halves[1 - part : 1 - part + back + 1][::-1])
        has = got[part] = {0: mine, 2: swap(mine, 2), 4: swap(mine, 4)}
        has[6] = swap(has[4], 2) if part == 1 else swap(has[2], 4)
        for bits in (0, 2, 4, 6):
            has[bits | 1] = swap(has[bits], 1)
    for part in (1, 0):
        pieces = lambda *bits: [(b, got[part][b]) for b in bits]
        acc = None
        for bits in ((0, 1), (2, 3, 4, 5), (6,)):
            acc = product(out_weight, pieces(*bits), acc)
        out = store(part, out_weight, pieces(7), acc, out)
    return out


def solution(mesh):
    return jax.shard_map(
        shards,
        mesh=mesh,
        in_specs=(P("seq", None), P(), P(None, "tp"), P(None, "tp"), P(None, "tp"), P(None, "tp"), P()),
        out_specs=P("seq", "tp"),
        check_vma=False,
    )
```

profile of v0, /device:TPU:0, one launch (start us, length us, event | category | flops | bytes accessed | tf_op | source)
XLA Modules:
  0.0 50.9 jit_solution(8209725438096005723)
XLA Ops:
  0.0 3.9 %second_half.1 = (bf16[256,256]{1,0:T(8,128)(2,1)S(1)}, bf16[256,4096]{1,0:T(8,128)(2,1)S(1)}, bf16[4096,256]{1,0:T(8,128)(2,1)S(1)}, bf16[256,4096]{1,0:T(8,128...) custom-call(bf16[512,4096]{1,0:T(8,128)(2,1)} %tokens.1, f32[1,4096]{1,0:T(1,128)} %bitcast.1, ...), custom_call_target="tpu_custom_call" | custom-call | tf_op jit(solution)/shard_map/second_half/pallas_call | solution.py:116
  3.9 3.1 %collective-permute-start.2 = (bf16[256,256]{1,0:T(8,128)(2,1)S(1)}, bf16[256,256]{1,0:T(8,128)(2,1)S(1)}, u32[]{:S(2)}, u32[]{:S(2)}) collective-permute-start(bf16[256,256]{1,0:T(8,128)(2,1)S(1)} %get-tuple-element.23.refs_4_), channel_id=1, source_target_pairs={{0,8},{8,16},{16,24},{24,0},{1,9},{9,17},{17,25},{25,1},{2,10},{10... | collective-permute-start | bytes 393224 | tf_op jit(solution)/shard_map/ppermute | solution.py:303
  7.0 2.2 %first_half.1 = (bf16[256,256]{1,0:T(8,128)(2,1)S(1)}, bf16[256,4096]{1,0:T(8,128)(2,1)S(1)}, bf16[4096,512]{1,0:T(8,128)(2,1)S(1)}) custom-call(bf16[256,4096]{1,0:T(8,128)(2,1)S(1)} %get-tuple-element.15.tokens, f32[1,4096]{1,0:T(1,128)S(1)} %get-tuple-element.16.gain, bf16[4096,256]{1,0:T(8,128)(2,1)S(1)} %get-tuple-element.17.weight, ...), custom_call_target="tpu_custom_call" | custom-call | tf_op jit(solution)/shard_map/first_half/pallas_call | solution.py:148
  9.2 0.0 copy-start.1
  9.2 0.0 copy-start.2
  9.2 1.6 %collective-permute-start = (bf16[256,256]{1,0:T(8,128)(2,1)S(1)}, bf16[256,256]{1,0:T(8,128)(2,1)S(1)}, u32[]{:S(2)}, u32[]{:S(2)}) collective-permute-start(bf16[256,256]{1,0:T(8,128)(2,1)S(1)} %get-tuple-element.22.refs_4_.refs_3_), channel_id=1, source_target_pairs={{0,8},{8,16},{16,24},{24,0},{1,9},{9,17},{17,25},{25,1},{2,10},{10... | collective-permute-start | bytes 393224 | tf_op jit(solution)/shard_map/ppermute | solution.py:303
  10.8 1.7 %collective-permute-done.2.refs_3_.refs_2_ = bf16[256,256]{1,0:T(8,128)(2,1)S(1)} collective-permute-done((bf16[256,256]{1,0:T(8,128)(2,1)S(1)}, bf16[256,256]{1,0:T(8,128)(2,1)S(1)}, u32[]{:S(2)}, u32[]{:S(2)}) %collective-permute-start.2) | collective-permute-done | bytes 131104 | tf_op jit(solution)/shard_map/ppermute | solution.py:303
  12.5 0.0 collective-permute-start.3
  12.5 3.5 %collective-permute-done.refs_2_.refs_1_ = bf16[256,256]{1,0:T(8,128)(2,1)S(1)} collective-permute-done((bf16[256,256]{1,0:T(8,128)(2,1)S(1)}, bf16[256,256]{1,0:T(8,128)(2,1)S(1)}, u32[]{:S(2)}, u32[]{:S(2)}) %collective-permute-start) | collective-permute-done | bytes 131104 | tf_op jit(solution)/shard_map/ppermute | solution.py:303
  16.0 0.9 %collective-permute-start.1 = (bf16[256,256]{1,0:T(8,128)(2,1)S(1)}, bf16[256,256]{1,0:T(8,128)(2,1)S(1)}, u32[]{:S(2)}, u32[]{:S(2)}) collective-permute-start(bf16[256,256]{1,0:T(8,128)(2,1)S(1)} %collective-permute-done.refs_2_.refs_1_), channel_id=1, source_target_pairs={{0,8},{8,16},{16,24},{24,0},{1,9},{9,17},{17,25},{25,1},{2,10},{10... | collective-permute-start | bytes 393224 | tf_op jit(solution)/shard_map/ppermute | solution.py:303
  17.0 1.4 %shard_map.123.q_ref = bf16[256,512]{1,0:T(8,128)(2,1)S(1)} custom-call(bf16[256,4096]{1,0:T(8,128)(2,1)S(1)} %get-tuple-element.24.normed, bf16[4096,512]{1,0:T(8,128)(2,1)S(1)} %get-tuple-element.21.weight, f32[512,128]{1,0:T(8,128)S(1)} %get-tuple-element.18.cosine, f32[512,128]{1,0:T(8,128)S(1)} %get-tuple-element.19.sine), custom_call_target="tpu_custom_call" | custom-call | tf_op jit(solution)/shard_map/pallas_call | solution.py:171
  18.4 0.0 copy-done.1
  18.4 0.0 copy-done.2
  18.4 0.2 fusion.limits
  18.6 1.1 %collective-permute-done.3.refs_1_.refs_0_ = bf16[256,256]{1,0:T(8,128)(2,1)S(1)} collective-permute-done((bf16[256,256]{1,0:T(8,128)(2,1)S(1)}, bf16[256,256]{1,0:T(8,128)(2,1)S(1)}, u32[]{:S(2)}, u32[]{:S(2)}) %collective-permute-start.3) | collective-permute-done | bytes 131104 | tf_op jit(solution)/shard_map/ppermute | solution.py:303
  19.7 2.9 %shard_map.124.refs_0_ = bf16[256,512]{1,0:T(8,128)(2,1)S(1)} custom-call(s32[2]{0:T(128)S(1)} %fusion.limits, bf16[256,512]{1,0:T(8,128)(2,1)S(1)} %shard_map.123.q_ref, bf16[256,256]{1,0:T(8,128)(2,1)S(1)} %collective-permute-done.3.refs_1_.refs_0_, bf16[256,256]{1,0:T(8,128)(2,1)S(1)} %collective-permute-done.refs_2_.refs_1_, ...), custom_call_target="tpu_custom_call" | custom-call | tf_op jit(solution)/shard_map/pallas_call | solution.py:224
  22.6 0.0 copy-start
  22.6 0.1 collective-permute-start.17
  22.7 1.6 %collective-permute-start.14 = (bf16[256,512]{1,0:T(8,128)(2,1)S(1)}, bf16[256,512]{1,0:T(8,128)(2,1)S(1)}, u32[]{:S(2)}, u32[]{:S(2)}) collective-permute-start(bf16[256,512]{1,0:T(8,128)(2,1)S(1)} %shard_map.124.refs_0_), channel_id=1, source_target_pairs={{0,2},{1,3},{2,0},{3,1},{4,6},{5,7},{6,4},{7,5},{8,10},{9,11},{10,... | collective-permute-start | bytes 786440 | tf_op jit(solution)/shard_map/ppermute | solution.py:308
  24.2 1.4 %shard_map.118.q_ref = bf16[256,512]{1,0:T(8,128)(2,1)S(1)} custom-call(bf16[256,4096]{1,0:T(8,128)(2,1)S(1)} %get-tuple-element.20.normed, bf16[4096,512]{1,0:T(8,128)(2,1)S(1)} %get-tuple-element.21.weight, f32[512,128]{1,0:T(8,128)S(1)} %get-tuple-element.18.cosine, f32[512,128]{1,0:T(8,128)S(1)} %get-tuple-element.19.sine), custom_call_target="tpu_custom_call" | custom-call | tf_op jit(solution)/shard_map/pallas_call | solution.py:171
  25.6 1.6 %collective-permute-start.11 = (bf16[256,512]{1,0:T(8,128)(2,1)S(1)}, bf16[256,512]{1,0:T(8,128)(2,1)S(1)}, u32[]{:S(2)}, u32[]{:S(2)}) collective-permute-start(bf16[256,512]{1,0:T(8,128)(2,1)S(1)} %shard_map.124.refs_0_), channel_id=1, source_target_pairs={{0,4},{1,5},{2,6},{3,7},{4,0},{5,1},{6,2},{7,3},{8,12},{9,13},{10,... | collective-permute-start | bytes 786440 | tf_op jit(solution)/shard_map/ppermute | solution.py:308
  27.2 0.0 collective-permute-done.1.refs_0_
  27.2 2.8 %shard_map.119.refs_0_ = bf16[256,512]{1,0:T(8,128)(2,1)S(1)} custom-call(s32[2]{0:T(128)S(1)} %fusion.limits, bf16[256,512]{1,0:T(8,128)(2,1)S(1)} %shard_map.118.q_ref, bf16[256,256]{1,0:T(8,128)(2,1)S(1)} %collective-permute-done.1.refs_0_, bf16[256,256]{1,0:T(8,128)(2,1)S(1)} %collective-permute-done.3.refs_1_.refs_0_, ...), custom_call_target="tpu_custom_call" | custom-call | tf_op jit(solution)/shard_map/pallas_call | solution.py:224
  30.1 0.6 %collective-permute-start.4 = (bf16[256,512]{1,0:T(8,128)(2,1)S(1)}, bf16[256,512]{1,0:T(8,128)(2,1)S(1)}, u32[]{:S(2)}, u32[]{:S(2)}) collective-permute-start(bf16[256,512]{1,0:T(8,128)(2,1)S(1)} %shard_map.119.refs_0_), channel_id=1, source_target_pairs={{0,2},{1,3},{2,0},{3,1},{4,6},{5,7},{6,4},{7,5},{8,10},{9,11},{10,... | collective-permute-start | bytes 786440 | tf_op jit(solution)/shard_map/ppermute | solution.py:308
  30.7 0.0 collective-permute-start.10
  30.7 0.0 collective-permute-done.17.refs_1_
  30.7 0.5 collective-permute-start.8
  31.2 0.2 collective-permute-done.14.refs_0_
  31.4 0.0 collective-permute-start.15
  31.4 2.9 %collective-permute-done.11.refs_2_ = bf16[256,512]{1,0:T(8,128)(2,1)S(1)} collective-permute-done((bf16[256,512]{1,0:T(8,128)(2,1)S(1)}, bf16[256,512]{1,0:T(8,128)(2,1)S(1)}, u32[]{:S(2)}, u32[]{:S(2)}) %collective-permute-start.11) | collective-permute-done | bytes 262176 | tf_op jit(solution)/shard_map/ppermute | solution.py:308
  34.4 0.2 collective-permute-start.12
  34.6 4.7 %collective-permute-done.4.refs_0_ = bf16[256,512]{1,0:T(8,128)(2,1)S(1)} collective-permute-done((bf16[256,512]{1,0:T(8,128)(2,1)S(1)}, bf16[256,512]{1,0:T(8,128)(2,1)S(1)}, u32[]{:S(2)}, u32[]{:S(2)}) %collective-permute-start.4) | collective-permute-done | bytes 262176 | tf_op jit(solution)/shard_map/ppermute | solution.py:308
  39.3 0.5 collective-permute-start.5
  39.8 0.0 collective-permute-done.10.refs_1_
  39.8 0.0 collective-permute-start.16
  39.8 0.0 collective-permute-done.8.refs_2_
  39.8 0.5 collective-permute-start.7
  40.3 0.0 collective-permute-done.15.refs_1_
  40.3 0.1 collective-permute-start.9
  40.4 3.4 %collective-permute-done.12.refs_0_ = bf16[256,512]{1,0:T(8,128)(2,1)S(1)} collective-permute-done((bf16[256,512]{1,0:T(8,128)(2,1)S(1)}, bf16[256,512]{1,0:T(8,128)(2,1)S(1)}, u32[]{:S(2)}, u32[]{:S(2)}) %collective-permute-start.12) | collective-permute-done | bytes 262176 | tf_op jit(solution)/shard_map/ppermute | solution.py:308
  43.8 0.0 collective-permute-start.13
  43.8 1.8 %collective-permute-done.5.refs_0_ = bf16[256,512]{1,0:T(8,128)(2,1)S(1)} collective-permute-done((bf16[256,512]{1,0:T(8,128)(2,1)S(1)}, bf16[256,512]{1,0:T(8,128)(2,1)S(1)}, u32[]{:S(2)}, u32[]{:S(2)}) %collective-permute-start.5) | collective-permute-done | bytes 262176 | tf_op jit(solution)/shard_map/ppermute | solution.py:308
  45.7 0.0 collective-permute-start.6
  45.7 0.0 copy-done
  45.7 0.4 shard_map.125.refs_4_
  46.1 0.4 shard_map.120.refs_4_
  46.6 0.0 collective-permute-done.16.refs_3_
  46.6 0.7 %shard_map.126.refs_1_ = f32[256,512]{1,0:T(8,128)S(1)} custom-call(bf16[4096,512]{1,0:T(8,128)(2,1)S(1)} %copy-done, bf16[256,512]{1,0:T(8,128)(2,1)S(1)} %collective-permute-done.14.refs_0_, bf16[256,512]{1,0:T(8,128)(2,1)S(1)} %collective-permute-done.15.refs_1_, bf16[256,512]{1,0:T(8,128)(2,1)S(1)} %collective-permute-done.11.refs_2_, ...), custom_call_target="tpu_custom_call" | custom-call | tf_op jit(solution)/shard_map/pallas_call | solution.py:252
  47.3 0.3 shard_map.127.refs_1_
  47.6 0.0 collective-permute-done.7.refs_1_
  47.6 0.0 collective-permute-done.9.refs_3_
  47.6 0.7 %shard_map.121.refs_1_ = f32[256,512]{1,0:T(8,128)S(1)} custom-call(bf16[4096,512]{1,0:T(8,128)(2,1)S(1)} %copy-done, bf16[256,512]{1,0:T(8,128)(2,1)S(1)} %collective-permute-done.4.refs_0_, bf16[256,512]{1,0:T(8,128)(2,1)S(1)} %collective-permute-done.7.refs_1_, bf16[256,512]{1,0:T(8,128)(2,1)S(1)} %collective-permute-done.8.refs_2_, ...), custom_call_target="tpu_custom_call" | custom-call | tf_op jit(solution)/shard_map/pallas_call | solution.py:252
  48.4 0.3 shard_map.122.refs_1_
  48.7 0.0 collective-permute-done.13.refs_0_
  48.7 1.0 %shard_map.128.refs_2_ = bf16[512,512]{1,0:T(8,128)(2,1)} custom-call(bf16[4096,512]{1,0:T(8,128)(2,1)S(1)} %copy-done, bf16[256,512]{1,0:T(8,128)(2,1)S(1)} %collective-permute-done.13.refs_0_, f32[256,512]{1,0:T(8,128)S(1)} %shard_map.127.refs_1_), custom_call_target="tpu_custom_call" | custom-call | tf_op jit(solution)/shard_map/pallas_call | solution.py:276
  49.7 0.0 collective-permute-done.6.refs_0_
  49.7 1.0 %shard_map.129 = bf16[512,512]{1,0:T(8,128)(2,1)} custom-call(bf16[4096,512]{1,0:T(8,128)(2,1)S(1)} %copy-done, bf16[256,512]{1,0:T(8,128)(2,1)S(1)} %collective-permute-done.6.refs_0_, f32[256,512]{1,0:T(8,128)S(1)} %shard_map.122.refs_1_, bf16[512,512]{1,0:T(8,128)(2,1)} %shard_map.128.refs_2_), custom_call_target="tpu_custom_call", output_to_operand_aliasing={{}: (3, {})} | custom-call | tf_op jit(solution)/shard_map/pallas_call | solution.py:276
Async XLA Ops:
  3.9 8.6 %collective-permute-start.2 = (bf16[256,256]{1,0:T(8,128)(2,1)S(1)}, bf16[256,256]{1,0:T(8,128)(2,1)S(1)}, u32[]{:S(2)}, u32[]{:S(2)}) collective-permute-start(bf16[256,256]{1,0:T(8,128)(2,1)S(1)} %get-tuple-element.23.refs_4_), channel_id=1, source_target_pairs={{0,8},{8,16},{16,24},{24,0},{1,9},{9,17},{17,25},{25,1},{2,10},{10... | collective-permute-start | bytes 393224 | tf_op jit(solution)/shard_map/ppermute | solution.py:303
  9.2 9.2 %copy-start.1 = (s32[2048]{0:T(1024)S(1)}, s32[2048]{0:T(1024)}, u32[]{:S(2)}) copy-start(s32[2048]{0:T(1024)} %param.18) | copy-start | bytes 24580
  9.2 9.2 %copy-start.2 = (s32[2]{0:T(128)S(1)}, s32[2]{0:T(128)}, u32[]{:S(2)}) copy-start(s32[2]{0:T(128)} %constant.17) | copy-start | bytes 28
  9.2 6.8 %collective-permute-start = (bf16[256,256]{1,0:T(8,128)(2,1)S(1)}, bf16[256,256]{1,0:T(8,128)(2,1)S(1)}, u32[]{:S(2)}, u32[]{:S(2)}) collective-permute-start(bf16[256,256]{1,0:T(8,128)(2,1)S(1)} %get-tuple-element.22.refs_4_.refs_3_), channel_id=1, source_target_pairs={{0,8},{8,16},{16,24},{24,0},{1,9},{9,17},{17,25},{25,1},{2,10},{10... | collective-permute-start | bytes 393224 | tf_op jit(solution)/shard_map/ppermute | solution.py:303
  12.5 7.2 %collective-permute-start.3 = (bf16[256,256]{1,0:T(8,128)(2,1)S(1)}, bf16[256,256]{1,0:T(8,128)(2,1)S(1)}, u32[]{:S(2)}, u32[]{:S(2)}) collective-permute-start(bf16[256,256]{1,0:T(8,128)(2,1)S(1)} %collective-permute-done.2.refs_3_.refs_2_), channel_id=1, source_target_pairs={{0,8},{8,16},{16,24},{24,0},{1,9},{9,17},{17,25},{25,1},{2,10},{10... | collective-permute-start | bytes 393224 | tf_op jit(solution)/shard_map/ppermute | solution.py:303
  16.0 11.2 %collective-permute-start.1 = (bf16[256,256]{1,0:T(8,128)(2,1)S(1)}, bf16[256,256]{1,0:T(8,128)(2,1)S(1)}, u32[]{:S(2)}, u32[]{:S(2)}) collective-permute-start(bf16[256,256]{1,0:T(8,128)(2,1)S(1)} %collective-permute-done.refs_2_.refs_1_), channel_id=1, source_target_pairs={{0,8},{8,16},{16,24},{24,0},{1,9},{9,17},{17,25},{25,1},{2,10},{10... | collective-permute-start | bytes 393224 | tf_op jit(solution)/shard_map/ppermute | solution.py:303
  22.6 23.1 %copy-start = (bf16[4096,512]{1,0:T(8,128)(2,1)S(1)}, bf16[4096,512]{1,0:T(8,128)(2,1)}, u32[]{:S(2)}) copy-start(bf16[4096,512]{1,0:T(8,128)(2,1)} %weight.15) | copy-start | bytes 12582916
  22.6 8.1 %collective-permute-start.17 = (bf16[256,512]{1,0:T(8,128)(2,1)S(1)}, bf16[256,512]{1,0:T(8,128)(2,1)S(1)}, u32[]{:S(2)}, u32[]{:S(2)}) collective-permute-start(bf16[256,512]{1,0:T(8,128)(2,1)S(1)} %shard_map.124.refs_0_), channel_id=1, source_target_pairs={{0,1},{1,0},{2,3},{3,2},{4,5},{5,4},{6,7},{7,6},{8,9},{9,8},{10,11... | collective-permute-start | bytes 786440 | tf_op jit(solution)/shard_map/ppermute | solution.py:308
  22.7 8.7 %collective-permute-start.14 = (bf16[256,512]{1,0:T(8,128)(2,1)S(1)}, bf16[256,512]{1,0:T(8,128)(2,1)S(1)}, u32[]{:S(2)}, u32[]{:S(2)}) collective-permute-start(bf16[256,512]{1,0:T(8,128)(2,1)S(1)} %shard_map.124.refs_0_), channel_id=1, source_target_pairs={{0,2},{1,3},{2,0},{3,1},{4,6},{5,7},{6,4},{7,5},{8,10},{9,11},{10,... | collective-permute-start | bytes 786440 | tf_op jit(solution)/shard_map/ppermute | solution.py:308
  25.6 8.7 %collective-permute-start.11 = (bf16[256,512]{1,0:T(8,128)(2,1)S(1)}, bf16[256,512]{1,0:T(8,128)(2,1)S(1)}, u32[]{:S(2)}, u32[]{:S(2)}) collective-permute-start(bf16[256,512]{1,0:T(8,128)(2,1)S(1)} %shard_map.124.refs_0_), channel_id=1, source_target_pairs={{0,4},{1,5},{2,6},{3,7},{4,0},{5,1},{6,2},{7,3},{8,12},{9,13},{10,... | collective-permute-start | bytes 786440 | tf_op jit(solution)/shard_map/ppermute | solution.py:308
  30.1 9.2 %collective-permute-start.4 = (bf16[256,512]{1,0:T(8,128)(2,1)S(1)}, bf16[256,512]{1,0:T(8,128)(2,1)S(1)}, u32[]{:S(2)}, u32[]{:S(2)}) collective-permute-start(bf16[256,512]{1,0:T(8,128)(2,1)S(1)} %shard_map.119.refs_0_), channel_id=1, source_target_pairs={{0,2},{1,3},{2,0},{3,1},{4,6},{5,7},{6,4},{7,5},{8,10},{9,11},{10,... | collective-permute-start | bytes 786440 | tf_op jit(solution)/shard_map/ppermute | solution.py:308
  30.7 9.2 %collective-permute-start.10 = (bf16[256,512]{1,0:T(8,128)(2,1)S(1)}, bf16[256,512]{1,0:T(8,128)(2,1)S(1)}, u32[]{:S(2)}, u32[]{:S(2)}) collective-permute-start(bf16[256,512]{1,0:T(8,128)(2,1)S(1)} %shard_map.119.refs_0_), channel_id=1, source_target_pairs={{0,1},{1,0},{2,3},{3,2},{4,5},{5,4},{6,7},{7,6},{8,9},{9,8},{10,11... | collective-permute-start | bytes 786440 | tf_op jit(solution)/shard_map/ppermute | solution.py:308
  30.7 9.2 %collective-permute-start.8 = (bf16[256,512]{1,0:T(8,128)(2,1)S(1)}, bf16[256,512]{1,0:T(8,128)(2,1)S(1)}, u32[]{:S(2)}, u32[]{:S(2)}) collective-permute-start(bf16[256,512]{1,0:T(8,128)(2,1)S(1)} %shard_map.119.refs_0_), channel_id=1, source_target_pairs={{0,4},{1,5},{2,6},{3,7},{4,0},{5,1},{6,2},{7,3},{8,12},{9,13},{10,... | collective-permute-start | bytes 786440 | tf_op jit(solution)/shard_map/ppermute | solution.py:308
  31.4 8.9 %collective-permute-start.15 = (bf16[256,512]{1,0:T(8,128)(2,1)S(1)}, bf16[256,512]{1,0:T(8,128)(2,1)S(1)}, u32[]{:S(2)}, u32[]{:S(2)}) collective-permute-start(bf16[256,512]{1,0:T(8,128)(2,1)S(1)} %collective-permute-done.14.refs_0_), channel_id=1, source_target_pairs={{0,1},{1,0},{2,3},{3,2},{4,5},{5,4},{6,7},{7,6},{8,9},{9,8},{10,11... | collective-permute-start | bytes 786440 | tf_op jit(solution)/shard_map/ppermute | solution.py:308
  34.4 9.5 %collective-permute-start.12 = (bf16[256,512]{1,0:T(8,128)(2,1)S(1)}, bf16[256,512]{1,0:T(8,128)(2,1)S(1)}, u32[]{:S(2)}, u32[]{:S(2)}) collective-permute-start(bf16[256,512]{1,0:T(8,128)(2,1)S(1)} %collective-permute-done.11.refs_2_), channel_id=1, source_target_pairs={{0,2},{1,3},{2,0},{3,1},{4,6},{5,7},{6,4},{7,5},{8,10},{9,11},{10,... | collective-permute-start | bytes 786440 | tf_op jit(solution)/shard_map/ppermute | solution.py:308
  39.3 6.4 %collective-permute-start.5 = (bf16[256,512]{1,0:T(8,128)(2,1)S(1)}, bf16[256,512]{1,0:T(8,128)(2,1)S(1)}, u32[]{:S(2)}, u32[]{:S(2)}) collective-permute-start(bf16[256,512]{1,0:T(8,128)(2,1)S(1)} %collective-permute-done.4.refs_0_), channel_id=1, source_target_pairs={{0,4},{1,5},{2,6},{3,7},{4,0},{5,1},{6,2},{7,3},{8,12},{9,13},{10,... | collective-permute-start | bytes 786440 | tf_op jit(solution)/shard_map/ppermute | solution.py:308
  39.8 6.8 %collective-permute-start.16 = (bf16[256,512]{1,0:T(8,128)(2,1)S(1)}, bf16[256,512]{1,0:T(8,128)(2,1)S(1)}, u32[]{:S(2)}, u32[]{:S(2)}) collective-permute-start(bf16[256,512]{1,0:T(8,128)(2,1)S(1)} %collective-permute-done.11.refs_2_), channel_id=1, source_target_pairs={{0,1},{1,0},{2,3},{3,2},{4,5},{5,4},{6,7},{7,6},{8,9},{9,8},{10,11... | collective-permute-start | bytes 786440 | tf_op jit(solution)/shard_map/ppermute | solution.py:308
  39.8 7.8 %collective-permute-start.7 = (bf16[256,512]{1,0:T(8,128)(2,1)S(1)}, bf16[256,512]{1,0:T(8,128)(2,1)S(1)}, u32[]{:S(2)}, u32[]{:S(2)}) collective-permute-start(bf16[256,512]{1,0:T(8,128)(2,1)S(1)} %collective-permute-done.4.refs_0_), channel_id=1, source_target_pairs={{0,1},{1,0},{2,3},{3,2},{4,5},{5,4},{6,7},{7,6},{8,9},{9,8},{10,11... | collective-permute-start | bytes 786440 | tf_op jit(solution)/shard_map/ppermute | solution.py:308
  40.3 7.3 %collective-permute-start.9 = (bf16[256,512]{1,0:T(8,128)(2,1)S(1)}, bf16[256,512]{1,0:T(8,128)(2,1)S(1)}, u32[]{:S(2)}, u32[]{:S(2)}) collective-permute-start(bf16[256,512]{1,0:T(8,128)(2,1)S(1)} %collective-permute-done.8.refs_2_), channel_id=1, source_target_pairs={{0,1},{1,0},{2,3},{3,2},{4,5},{5,4},{6,7},{7,6},{8,9},{9,8},{10,11... | collective-permute-start | bytes 786440 | tf_op jit(solution)/shard_map/ppermute | solution.py:308
  43.8 4.8 %collective-permute-start.13 = (bf16[256,512]{1,0:T(8,128)(2,1)S(1)}, bf16[256,512]{1,0:T(8,128)(2,1)S(1)}, u32[]{:S(2)}, u32[]{:S(2)}) collective-permute-start(bf16[256,512]{1,0:T(8,128)(2,1)S(1)} %collective-permute-done.12.refs_0_), channel_id=1, source_target_pairs={{0,1},{1,0},{2,3},{3,2},{4,5},{5,4},{6,7},{7,6},{8,9},{9,8},{10,11... | collective-permute-start | bytes 786440 | tf_op jit(solution)/shard_map/ppermute | solution.py:308
  45.7 4.0 %collective-permute-start.6 = (bf16[256,512]{1,0:T(8,128)(2,1)S(1)}, bf16[256,512]{1,0:T(8,128)(2,1)S(1)}, u32[]{:S(2)}, u32[]{:S(2)}) collective-permute-start(bf16[256,512]{1,0:T(8,128)(2,1)S(1)} %collective-permute-done.5.refs_0_), channel_id=1, source_target_pairs={{0,1},{1,0},{2,3},{3,2},{4,5},{5,4},{6,7},{7,6},{8,9},{9,8},{10,11... | collective-permute-start | bytes 786440 | tf_op jit(solution)/shard_map/ppermute | solution.py:308
where the time goes:
time: 51.1 us; the launch traced here: 50.9 us
  Pallas kernels  19.5 us (38%)
  waiting for transfers between devices  19.5 us (38%)
  starting transfers between devices  11.3 us (22%)
    ppermute x14, waiting for transfers between devices, swap(): return lax.ppermute(x, 'tp', [(i, i ^ bit) for i in range(tp_count)])  13.2 us
    ppermute x4, waiting for transfers between devices, shards(): halves[distance] = lax.ppermute(halves[distance - 2], 'seq', ring)  6.31 us
    pallas_call x2, Pallas kernels, attend(): pl.pallas_call(functools.partial(attend_kernel, part, back), out_shape=ja...  5.73 us
    ppermute x4, starting transfers between devices, shards(): halves[distance] = lax.ppermute(halves[distance - 2], 'seq', ring)  5.68 us
    ppermute x14, starting transfers between devices, swap(): return lax.ppermute(x, 'tp', [(i, i ^ bit) for i in range(tp_count)])  5.66 us
    pallas_call x1, Pallas kernels, second_half(): pl.pallas_call(functools.partial(second_half_kernel, tile), out_shape=(sh...  3.85 us
    pallas_call x6, Pallas kernels, product(): pl.pallas_call(functools.partial(product_kernel, bits, bool(extra)), out_...  2.91 us
    pallas_call x2, Pallas kernels, query(): pl.pallas_call(functools.partial(query_kernel, part), out_shape=jax.Shape...  2.76 us
  transfers between devices with their start and end apart: 18, of which 8 were waited for; matrix products, arithmetic and copies ran while one was open for 0% of the time, Pallas kernels for 29%

commit v1 on v0

--- a/solution.py
+++ b/solution.py
@@ -55,9 +55,9 @@
 
 
 def second_half_kernel(
-    tile, tokens, gain, key_weight, value_weight, row_cos, row_sin, start_cos, start_sin,
-    kv_ref, normed_ref, weight, first_tokens, gain_copy, cosine, sine,
-    held, row_c, row_s, start_c, start_s, tile_sems, sems,
+    tile, tokens, gain, key_weight, value_weight, row_cos, row_sin, start_cos, start_sin, segments,
+    kv_ref, normed_ref, weight, first_tokens, gain_copy, cosine, sine, limits,
+    held, row_c, row_s, start_c, start_s, numbers, tile_sems, sems,
 ):
     rows, width = kv_ref.shape[0], key_weight.shape[1]
     steps = rows // tile
@@ -78,16 +78,16 @@
         (start_cos, start_c),
         (start_sin, start_s),
         (tokens.at[:rows, :], first_tokens),
+        (segments, numbers),
     ]
     moves = [pltpu.make_async_copy(a, b, sems.at[i]) for i, (a, b) in enumerate(moves)]
-    tiles[0].start()
-    moves[0].start()
-    for move in moves[1:3]:
+    for move in [moves[8], moves[0]] + tiles + moves[1:8]:
         move.start()
-    for copy in tiles[1:]:
-        copy.start()
-    for move in moves[3:]:
-        move.start()
+    moves[8].wait()
+    for value in (1, 2):
+        before = jnp.sum((numbers[...] < value).astype(jnp.float32), axis=0, keepdims=True)
+        count = jnp.broadcast_to(jnp.sum(before, axis=1, keepdims=True), before.shape)
+        limits[value - 1 : value, :] = count.astype(jnp.int32)
     moves[0].wait()
     for i in range(steps):
         here = slice(i * tile, (i + 1) * tile)
@@ -108,7 +108,7 @@
     moves[7].wait()
 
 
-def second_half(tokens, gain, key_weight, value_weight, tables):
+def second_half(tokens, gain, key_weight, value_weight, tables, segments):
     block_rows, depth = tokens.shape
     half, width = block_rows // 2, key_weight.shape[1]
     tile = min(half, 64)
@@ -123,41 +123,38 @@
             shape(gain.shape, f32),
             shape((block_rows, HEAD_DIM), f32),
             shape((block_rows, HEAD_DIM), f32),
+            shape((2, HEAD_DIM), jnp.int32),
         ),
-        in_specs=[HBM] * 8,
-        out_specs=(VMEM,) * 7,
+        in_specs=[HBM] * 9,
+        out_specs=(VMEM,) * 8,
         scratch_shapes=[pltpu.VMEM((half, depth), bf16)]
         + [pltpu.VMEM(t.shape, f32) for t in tables]
-        + [pltpu.SemaphoreType.DMA((half // tile,)), pltpu.SemaphoreType.DMA((8,))],
+        + [pltpu.VMEM(segments.shape, jnp.int32)]
+        + [pltpu.SemaphoreType.DMA((half // tile,)), pltpu.SemaphoreType.DMA((9,))],
         compiler_params=PARAMS,
         name="second_half",
-    )(*in_hbm(tokens, gain, key_weight, value_weight, *tables))
-
-
-def first_half_kernel(tokens, gain, weight, cosine, sine, query_weight, kv_ref, normed_ref, query_copy, sem):
-    move = pltpu.make_async_copy(query_weight, query_copy, sem)
-    move.start()
+    )(*in_hbm(tokens, gain, key_weight, value_weight, *tables, segments))
+
+
+def first_half_kernel(tokens, gain, weight, cosine, sine, kv_ref, normed_ref):
     rows = kv_ref.shape[0]
     normed_ref[...] = normalise(tokens[...], gain[...])
     key_value_of(normed_ref[...], weight[...], cosine[:rows, :], sine[:rows, :], kv_ref, slice(None))
-    move.wait()
-
-
-def first_half(tokens, gain, weight, cosine, sine, query_weight):
+
+
+def first_half(tokens, gain, weight, cosine, sine):
     half = tokens.shape[0]
     return pl.pallas_call(
         first_half_kernel,
         out_shape=(
             jax.ShapeDtypeStruct((half, weight.shape[1]), jnp.bfloat16),
             jax.ShapeDtypeStruct(tokens.shape, jnp.bfloat16),
-            jax.ShapeDtypeStruct(query_weight.shape, jnp.bfloat16),
         ),
-        in_specs=[VMEM] * 5 + [HBM],
-        out_specs=(VMEM,) * 3,
-        scratch_shapes=[pltpu.SemaphoreType.DMA],
+        in_specs=[VMEM] * 5,
+        out_specs=(VMEM,) * 2,
         compiler_params=PARAMS,
         name="first_half",
-    )(tokens, gain, weight, cosine, sine, *in_hbm(query_weight))
+    )(tokens, gain, weight, cosine, sine)
 
 
 def query_kernel(part, normed, weight, cosine, sine, out_ref):
@@ -177,58 +174,104 @@
     )(normed, weight, cosine, sine)
 
 
-def attend_kernel(part, back, limits, q_ref, *refs):
-    kv_refs, out_ref, bias_ref = refs[:-2], refs[-2], refs[-1]
-    rows, half = q_ref.shape[0], kv_refs[0].shape[0]
+TILE, AHEAD = 256, 3
+FACTOR = math.log2(math.e) / math.sqrt(HEAD_DIM)
+
+
+def bias_of(part, place, back, half, limits, bias_ref, column):
+    base = (2 * lax.axis_index("seq") + part) * half
+    row = base + lax.broadcasted_iota(jnp.int32, (half, HEAD_DIM), 0)
+    starts = [jnp.broadcast_to(limits[i : i + 1, :], row.shape) for i in range(2)]
+    start = jnp.where(row >= starts[1], starts[1], jnp.where(row >= starts[0], starts[0], 0))
+    start = jnp.maximum(start, row - (WINDOW - 1))
+    first = base - (back - place) * half
+    for left in range(0, half, HEAD_DIM):
+        key = first + left + lax.broadcasted_iota(jnp.int32, (half, HEAD_DIM), 1)
+        mask = key >= start
+        if place == back:
+            mask = mask & (key <= row)
+        bias_ref[:, column + left : column + left + HEAD_DIM] = jnp.where(
+            mask, jnp.float32(0), jnp.float32(-1e30)
+        )
+
+
+def attend_kernel(part, back, places, early, late, limits, q_ref, *refs):
+    kv_refs, refs = refs[: len(places)], refs[len(places) :]
+    bias_ref = refs[-1]
+    half = q_ref.shape[0]
     kv_width = kv_refs[0].shape[1] // 2
     group = q_ref.shape[1] // kv_width
-    factor = math.log2(math.e) / math.sqrt(HEAD_DIM)
-    places = [slice(p * half, (p + 1) * half) for p in range(back + 1)]
-    base = (2 * lax.axis_index("seq") + part) * half
-    row = base + lax.broadcasted_iota(jnp.int32, (rows, HEAD_DIM), 0)
-    start = jnp.where(row >= limits[1], limits[1], jnp.where(row >= limits[0], limits[0], 0))
-    start = jnp.maximum(start, row - (WINDOW - 1))
-    for place, span in enumerate(places):
-        first = base - (back - place) * half
-        for left in range(0, half, HEAD_DIM):
-            key = first + left + lax.broadcasted_iota(jnp.int32, (rows, HEAD_DIM), 1)
-            mask = key >= start
-            if place == back:
-                mask = mask & (key <= row)
-            bias_ref[:, place * half + left : place * half + left + HEAD_DIM] = jnp.where(
-                mask, jnp.float32(0), jnp.float32(-1e30)
+    for i, place in enumerate(places):
+        bias_of(part, place, back, half, limits, bias_ref, i * half)
+    ones = jnp.ones((half, HEAD_DIM), jnp.bfloat16)
+    tile = min(half, TILE)
+    wide = half // HEAD_DIM
+
+    def score(h, rows):
+        first = (h // group) * HEAD_DIM
+        q = q_ref[rows, h * HEAD_DIM : (h + 1) * HEAD_DIM]
+        scores = []
+        for i, kv in enumerate(kv_refs):
+            s = lax.dot_general(
+                q, kv[:, first : first + HEAD_DIM], (((1,), (1,)), ((), ())), preferred_element_type=jnp.float32
             )
-    ones = jnp.ones((half, HEAD_DIM), jnp.bfloat16)
-    for h, head in enumerate(heads_of(q_ref.shape[1])):
-        first = (h // group) * HEAD_DIM
-        keys, vals = slice(first, first + HEAD_DIM), slice(kv_width + first, kv_width + first + HEAD_DIM)
-        q = q_ref[:, head]
-        scores = [
-            lax.dot_general(q, kv[:, keys], (((1,), (1,)), ((), ())), preferred_element_type=jnp.float32)
-            * factor
-            + bias_ref[:, span]
-            for kv, span in zip(kv_refs, places)
-        ]
-        peak = jnp.max(functools.reduce(jnp.maximum, scores), axis=-1, keepdims=True)
+            scores.append(s * FACTOR + bias_ref[rows, i * half : (i + 1) * half])
+        return scores
+
+    def finish(h, rows, scores):
+        first = kv_width + (h // group) * HEAD_DIM
+        head = slice(h * HEAD_DIM, (h + 1) * HEAD_DIM)
+        pair = slice(2 * h * HEAD_DIM, 2 * (h + 1) * HEAD_DIM)
+        top = functools.reduce(jnp.maximum, scores)
+        top = functools.reduce(jnp.maximum, [top[:, c * HEAD_DIM : (c + 1) * HEAD_DIM] for c in range(wide)])
+        peak = jnp.broadcast_to(jnp.max(top, axis=-1, keepdims=True), top.shape)
         summed = 0.0
+        if late:
+            before = refs[1][rows, head]
+            peak = jnp.maximum(peak, before)
+            fade = jnp.exp2(before - peak)
+            summed = refs[0][rows, pair] * jnp.concatenate([fade, fade], axis=1)
+        peaks = jnp.concatenate([peak] * wide, axis=1)
         for s, kv in zip(scores, kv_refs):
-            w = jnp.exp2(s - peak).astype(jnp.bfloat16)
-            both = jnp.concatenate([kv[:, vals], ones], axis=1)
+            w = jnp.exp2(s - peaks).astype(jnp.bfloat16)
+            both = jnp.concatenate([kv[:, first : first + HEAD_DIM], ones], axis=1)
             summed = summed + jnp.dot(w, both, preferred_element_type=jnp.float32)
-        out_ref[:, head] = (summed[:, :HEAD_DIM] / summed[:, HEAD_DIM:]).astype(jnp.bfloat16)
-
-
-def attend(part, queries, limits, key_values):
-    half = queries.shape[0]
-    back = len(key_values) - 1
-    return pl.pallas_call(
-        functools.partial(attend_kernel, part, back),
-        out_shape=jax.ShapeDtypeStruct(queries.shape, jnp.bfloat16),
-        in_specs=[pl.BlockSpec(memory_space=pltpu.SMEM)] + [VMEM] * (1 + len(key_values)),
-        out_specs=VMEM,
-        scratch_shapes=[pltpu.VMEM((half, (back + 1) * half), jnp.float32)],
-        compiler_params=PARAMS,
-    )(limits, queries, *key_values)
+        if early:
+            refs[0][rows, pair] = summed
+            refs[1][rows, head] = peak
+        else:
+            refs[-2][rows, head] = (summed[:, :HEAD_DIM] / summed[:, HEAD_DIM:]).astype(jnp.bfloat16)
+
+    units = [
+        (h, slice(row, row + tile)) for h in range(q_ref.shape[1] // HEAD_DIM) for row in range(0, half, tile)
+    ]
+    waiting = []
+    for unit in units:
+        waiting.append((*unit, score(*unit)))
+        if len(waiting) > AHEAD:
+            finish(*waiting.pop(0))
+    for unit in waiting:
+        finish(*unit)
+
+
+def attend(part, back, places, queries, limits, key_values, early=False, before=()):
+    half, width = queries.shape
+    if early:
+        shape = (
+            jax.ShapeDtypeStruct((half, 2 * width), jnp.float32),
+            jax.ShapeDtypeStruct((half, width), jnp.float32),
+        )
+    else:
+        shape = jax.ShapeDtypeStruct((half, width), jnp.bfloat16)
+    key_values = [key_values[p] for p in places]
+    return pl.pallas_call(
+        functools.partial(attend_kernel, part, back, tuple(places), early, bool(before)),
+        out_shape=shape,
+        in_specs=[VMEM] * (2 + len(places) + len(before)),
+        out_specs=(VMEM, VMEM) if early else VMEM,
+        scratch_shapes=[pltpu.VMEM((half, len(places) * half), jnp.float32)],
+        compiler_params=pltpu.CompilerParams(vmem_limit_bytes=max(16, 2 * len(places)) << 20),
+    )(limits, queries, *key_values, *before)
 
 
 def added(bits, total, weight, xs):
@@ -292,26 +335,35 @@
     reach = min(WINDOW, total // 2)
     back = min((reach - 2) // half + 1, 2 * seq_count - 1)
     ring = [(i, (i + 1) % seq_count) for i in range(seq_count)]
-    limits = jnp.sum((segments[None, :] < jnp.array([[1], [2]], jnp.int32)).astype(jnp.int32), axis=1)
 
     halves, normed, queries = [None] * (back + 2), [None, None], [None, None]
-    halves[0], normed[1], weight, first_tokens, gain, cosine, sine = second_half(
-        tokens, norm_gain[None, :], key_weight, value_weight, rotation_tables(block_rows, seq_count)
+    halves[0], normed[1], weight, first_tokens, gain, cosine, sine, limits = second_half(
+        tokens,
+        norm_gain[None, :],
+        key_weight,
+        value_weight,
+        rotation_tables(block_rows, seq_count),
+        segments.reshape(-1, HEAD_DIM),
     )
-    halves[1], normed[0], query_copy = first_half(first_tokens, gain, weight, cosine, sine, query_weight)
+    halves[1], normed[0] = first_half(first_tokens, gain, weight, cosine, sine)
     for distance in range(2, back + 2):
         halves[distance] = lax.ppermute(halves[distance - 2], "seq", ring)
     for part in (1, 0):
-        queries[part] = query(part, normed[part], query_copy, cosine, sine)
+        queries[part] = query(part, normed[part], query_weight, cosine, sine)
 
     def swap(x, bit):
         return lax.ppermute(x, "tp", [(i, i ^ bit) for i in range(tp_count)])
 
     got, out = {}, None
     for part in (1, 0):
-        mine = attend(part, queries[part], limits, halves[1 - part : 1 - part + back + 1][::-1])
+        key_values = halves[1 - part : 1 - part + back + 1][::-1]
+        if part == 1:
+            before = attend(part, back, range(1, back + 1), queries[part], limits, key_values, early=True)
+            mine = attend(part, back, [0], queries[part], limits, key_values, before=before)
+        else:
+            mine = attend(part, back, range(back + 1), queries[part], limits, key_values)
         has = got[part] = {0: mine, 2: swap(mine, 2), 4: swap(mine, 4)}
-        has[6] = swap(has[4], 2) if part == 1 else swap(has[2], 4)
+        has[6] = swap(has[4], 2) if part == 0 else swap(has[2], 4)
         for bits in (0, 2, 4, 6):
             has[bits | 1] = swap(has[bits], 1)
     for part in (1, 0):

time: 51.1 us -> 55.3 us (1.082)
  waiting for transfers between devices: 19.5 us -> 24.7 us
  Pallas kernels: 19.5 us -> 17.3 us
  starting transfers between devices: 11.3 us -> 12.7 us
    ppermute x4, waiting for transfers between devices: 6.31 us -> 9.82 us  [shards(): halves[distance] = lax.ppermute(halves[distance - 2], 'seq', ring)]
    ppermute x14, starting transfers between devices: 5.66 us -> 7.88 us  [swap(): return lax.ppermute(x, 'tp', [(i, i ^ bit) for i in range(tp_count)])]
    ppermute x14, waiting for transfers between devices: 13.2 us -> 14.9 us  [swap(): return lax.ppermute(x, 'tp', [(i, i ^ bit) for i in range(tp_count)])]
    pallas_call x2 -> x3, Pallas kernels: 5.73 us -> 4.31 us  [attend(): pl.pallas_call(functools.partial(attend_kernel, part, back, tuple(places)...]
    ppermute x4, starting transfers between devices: 5.68 us -> 4.78 us  [shards(): halves[distance] = lax.ppermute(halves[distance - 2], 'seq', ring)]
    pallas_call x1, Pallas kernels: 2.2 us -> 1.41 us  [first_half(): pl.pallas_call(first_half_kernel, out_shape=(jax.ShapeDtypeStruct((half,...]
  transfers between devices with their start and end apart: 18 -> 18, of which waited for: 8 -> 8; matrix products, arithmetic and copies ran while one was open for 0% -> 0% of each run, Pallas kernels for 29% -> 16%
where the time goes in v1:
time: 55.3 us; the launch traced here: 55.1 us
  waiting for transfers between devices  24.7 us (45%)
  Pallas kernels  17.3 us (31%)
  starting transfers between devices  12.7 us (23%)
    ppermute x14, waiting for transfers between devices, swap(): return lax.ppermute(x, 'tp', [(i, i ^ bit) for i in range(tp_count)])  14.9 us
    ppermute x4, waiting for transfers between devices, shards(): halves[distance] = lax.ppermute(halves[distance - 2], 'seq', ring)  9.82 us
    ppermute x14, starting transfers between devices, swap(): return lax.ppermute(x, 'tp', [(i, i ^ bit) for i in range(tp_count)])  7.88 us
    ppermute x4, starting transfers between devices, shards(): halves[distance] = lax.ppermute(halves[distance - 2], 'seq', ring)  4.78 us
    pallas_call x3, Pallas kernels, attend(): pl.pallas_call(functools.partial(attend_kernel, part, back, tuple(places)...  4.31 us
    pallas_call x1, Pallas kernels, second_half(): pl.pallas_call(functools.partial(second_half_kernel, tile), out_shape=(sh...  3.9 us
    pallas_call x6, Pallas kernels, product(): pl.pallas_call(functools.partial(product_kernel, bits, bool(extra)), out_...  2.91 us
    pallas_call x2, Pallas kernels, query(): pl.pallas_call(functools.partial(query_kernel, part), out_shape=jax.Shape...  2.76 us
  transfers between devices with their start and end apart: 18, of which 8 were waited for; matrix products, arithmetic and copies ran while one was open for 0% of the time, Pallas kernels for 16%

profile of v1, /device:TPU:0, one launch (start us, length us, event | category | flops | bytes accessed | tf_op | source)
XLA Modules:
  0.0 55.1 jit_solution(17660515442888562948)
XLA Ops:
  0.0 3.9 %second_half.1 = (bf16[256,256]{1,0:T(8,128)(2,1)S(1)}, bf16[256,4096]{1,0:T(8,128)(2,1)S(1)}, bf16[4096,256]{1,0:T(8,128)(2,1)S(1)}, bf16[256,4096]{1,0:T(8,128...) custom-call(bf16[512,4096]{1,0:T(8,128)(2,1)} %tokens.1, ...), custom_call_target="tpu_custom_call" | custom-call | tf_op jit(solution)/shard_map/second_half/pallas_call | solution.py:116
  3.9 0.0 copy-start.1
  3.9 1.4 %first_half.1 = (bf16[256,256]{1,0:T(8,128)(2,1)S(1)}, bf16[256,4096]{1,0:T(8,128)(2,1)S(1)}) custom-call(bf16[256,4096]{1,0:T(8,128)(2,1)S(1)} %get-tuple-element.18.tokens, f32[1,4096]{1,0:T(1,128)S(1)} %get-tuple-element.19.gain, bf16[4096,256]{1,0:T(8,128)(2,1)S(1)} %get-tuple-element.20.weight, f32[512,128]{1,0:T(8,128)S(1)} %get-tuple-element.21.cosine, ...), custom_call_target="tpu_custom_call" | custom-call | tf_op jit(solution)/shard_map/first_half/pallas_call | solution.py:147
  5.3 3.1 %collective-permute-start = (bf16[256,256]{1,0:T(8,128)(2,1)S(1)}, bf16[256,256]{1,0:T(8,128)(2,1)S(1)}, u32[]{:S(2)}, u32[]{:S(2)}) collective-permute-start(bf16[256,256]{1,0:T(8,128)(2,1)S(1)} %get-tuple-element.24.refs_4_.refs_2_), channel_id=1, source_target_pairs={{0,8},{8,16},{16,24},{24,0},{1,9},{9,17},{17,25},{25,1},{2,10},{10... | collective-permute-start | bytes 393224 | tf_op jit(solution)/shard_map/ppermute | solution.py:350
  8.4 1.6 %collective-permute-start.2 = (bf16[256,256]{1,0:T(8,128)(2,1)S(1)}, bf16[256,256]{1,0:T(8,128)(2,1)S(1)}, u32[]{:S(2)}, u32[]{:S(2)}) collective-permute-start(bf16[256,256]{1,0:T(8,128)(2,1)S(1)} %get-tuple-element.25.refs_3_), channel_id=1, source_target_pairs={{0,8},{8,16},{16,24},{24,0},{1,9},{9,17},{17,25},{25,1},{2,10},{10... | collective-permute-start | bytes 393224 | tf_op jit(solution)/shard_map/ppermute | solution.py:350
  10.0 4.8 %collective-permute-done.refs_2_.refs_0_ = bf16[256,256]{1,0:T(8,128)(2,1)S(1)} collective-permute-done((bf16[256,256]{1,0:T(8,128)(2,1)S(1)}, bf16[256,256]{1,0:T(8,128)(2,1)S(1)}, u32[]{:S(2)}, u32[]{:S(2)}) %collective-permute-start) | collective-permute-done | bytes 131104 | tf_op jit(solution)/shard_map/ppermute | solution.py:350
  14.8 0.0 collective-permute-start.1
  14.8 2.0 %collective-permute-done.2.refs_3_.refs_1_ = bf16[256,256]{1,0:T(8,128)(2,1)S(1)} collective-permute-done((bf16[256,256]{1,0:T(8,128)(2,1)S(1)}, bf16[256,256]{1,0:T(8,128)(2,1)S(1)}, u32[]{:S(2)}, u32[]{:S(2)}) %collective-permute-start.2) | collective-permute-done | bytes 131104 | tf_op jit(solution)/shard_map/ppermute | solution.py:350
  16.8 0.1 collective-permute-start.3
  16.9 0.0 copy-done.1
  16.9 1.4 %shard_map.109.q_ref = bf16[256,512]{1,0:T(8,128)(2,1)S(1)} custom-call(bf16[256,4096]{1,0:T(8,128)(2,1)S(1)} %get-tuple-element.23.normed, bf16[4096,512]{1,0:T(8,128)(2,1)S(1)} %copy-done.1, f32[512,128]{1,0:T(8,128)S(1)} %get-tuple-element.21.cosine, f32[512,128]{1,0:T(8,128)S(1)} %get-tuple-element.22.sine), custom_call_target="tpu_custom_call" | custom-call | tf_op jit(solution)/shard_map/pallas_call | solution.py:168
  18.3 1.4 %shard_map.114.q_ref = bf16[256,512]{1,0:T(8,128)(2,1)S(1)} custom-call(bf16[256,4096]{1,0:T(8,128)(2,1)S(1)} %get-tuple-element.26.normed, bf16[4096,512]{1,0:T(8,128)(2,1)S(1)} %copy-done.1, f32[512,128]{1,0:T(8,128)S(1)} %get-tuple-element.21.cosine, f32[512,128]{1,0:T(8,128)S(1)} %get-tuple-element.22.sine), custom_call_target="tpu_custom_call" | custom-call | tf_op jit(solution)/shard_map/pallas_call | solution.py:168
  19.7 0.0 copy-start
  19.7 1.7 %shard_map.115 = (f32[256,1024]{1,0:T(8,128)S(1)}, f32[256,512]{1,0:T(8,128)S(1)}) custom-call(s32[2,128]{1,0:T(2,128)S(1)} %get-tuple-element.17.limits, bf16[256,512]{1,0:T(8,128)(2,1)S(1)} %shard_map.114.q_ref, bf16[256,256]{1,0:T(8,128)(2,1)S(1)} %collective-permute-done.refs_2_.refs_0_, bf16[256,256]{1,0:T(8,128)(2,1)S(1)} %collective-permute-done.2.refs_3_.refs_1_, ...), custom_call_target="tpu_custom_call" | custom-call | tf_op jit(solution)/shard_map/pallas_call | solution.py:267
  21.3 1.4 %collective-permute-done.1.refs_0_ = bf16[256,256]{1,0:T(8,128)(2,1)S(1)} collective-permute-done((bf16[256,256]{1,0:T(8,128)(2,1)S(1)}, bf16[256,256]{1,0:T(8,128)(2,1)S(1)}, u32[]{:S(2)}, u32[]{:S(2)}) %collective-permute-start.1) | collective-permute-done | bytes 131104 | tf_op jit(solution)/shard_map/ppermute | solution.py:350
  22.7 1.7 %collective-permute-done.3.refs_1_.refs_0_ = bf16[256,256]{1,0:T(8,128)(2,1)S(1)} collective-permute-done((bf16[256,256]{1,0:T(8,128)(2,1)S(1)}, bf16[256,256]{1,0:T(8,128)(2,1)S(1)}, u32[]{:S(2)}, u32[]{:S(2)}) %collective-permute-start.3) | collective-permute-done | bytes 131104 | tf_op jit(solution)/shard_map/ppermute | solution.py:350
  24.4 2.0 %shard_map.110.refs_0_ = bf16[256,512]{1,0:T(8,128)(2,1)S(1)} custom-call(s32[2,128]{1,0:T(2,128)S(1)} %get-tuple-element.17.limits, bf16[256,512]{1,0:T(8,128)(2,1)S(1)} %shard_map.109.q_ref, bf16[256,256]{1,0:T(8,128)(2,1)S(1)} %collective-permute-done.1.refs_0_, bf16[256,256]{1,0:T(8,128)(2,1)S(1)} %collective-permute-done.3.refs_1_.refs_0_, ...), custom_call_target="tpu_custom_call" | custom-call | tf_op jit(solution)/shard_map/pallas_call | solution.py:267
  26.4 0.1 collective-permute-start.10
  26.5 1.6 %collective-permute-start.7 = (bf16[256,512]{1,0:T(8,128)(2,1)S(1)}, bf16[256,512]{1,0:T(8,128)(2,1)S(1)}, u32[]{:S(2)}, u32[]{:S(2)}) collective-permute-start(bf16[256,512]{1,0:T(8,128)(2,1)S(1)} %shard_map.110.refs_0_), channel_id=1, source_target_pairs={{0,2},{1,3},{2,0},{3,1},{4,6},{5,7},{6,4},{7,5},{8,10},{9,11},{10,... | collective-permute-start | bytes 786440 | tf_op jit(solution)/shard_map/ppermute | solution.py:355
  28.1 0.6 %shard_map.116.refs_0_ = bf16[256,512]{1,0:T(8,128)(2,1)S(1)} custom-call(s32[2,128]{1,0:T(2,128)S(1)} %get-tuple-element.17.limits, bf16[256,512]{1,0:T(8,128)(2,1)S(1)} %shard_map.114.q_ref, bf16[256,256]{1,0:T(8,128)(2,1)S(1)} %collective-permute-done.3.refs_1_.refs_0_, f32[256,1024]{1,0:T(8,128)S(1)} %get-tuple-element.27.refs_1_, ...), custom_call_target="tpu_custom_call" | custom-call | tf_op jit(solution)/shard_map/pallas_call | solution.py:267
  28.7 0.6 %collective-permute-start.11 = (bf16[256,512]{1,0:T(8,128)(2,1)S(1)}, bf16[256,512]{1,0:T(8,128)(2,1)S(1)}, u32[]{:S(2)}, u32[]{:S(2)}) collective-permute-start(bf16[256,512]{1,0:T(8,128)(2,1)S(1)} %shard_map.116.refs_0_), channel_id=1, source_target_pairs={{0,2},{1,3},{2,0},{3,1},{4,6},{5,7},{6,4},{7,5},{8,10},{9,11},{10,... | collective-permute-start | bytes 786440 | tf_op jit(solution)/shard_map/ppermute | solution.py:355
  29.3 1.6 %collective-permute-start.4 = (bf16[256,512]{1,0:T(8,128)(2,1)S(1)}, bf16[256,512]{1,0:T(8,128)(2,1)S(1)}, u32[]{:S(2)}, u32[]{:S(2)}) collective-permute-start(bf16[256,512]{1,0:T(8,128)(2,1)S(1)} %shard_map.110.refs_0_), channel_id=1, source_target_pairs={{0,4},{1,5},{2,6},{3,7},{4,0},{5,1},{6,2},{7,3},{8,12},{9,13},{10,... | collective-permute-start | bytes 786440 | tf_op jit(solution)/shard_map/ppermute | solution.py:355
  30.9 0.0 collective-permute-start.17
  30.9 0.0 collective-permute-done.10.refs_1_
  30.9 0.5 collective-permute-start.15
  31.3 4.4 %collective-permute-done.7.refs_0_ = bf16[256,512]{1,0:T(8,128)(2,1)S(1)} collective-permute-done((bf16[256,512]{1,0:T(8,128)(2,1)S(1)}, bf16[256,512]{1,0:T(8,128)(2,1)S(1)}, u32[]{:S(2)}, u32[]{:S(2)}) %collective-permute-start.7) | collective-permute-done | bytes 262176 | tf_op jit(solution)/shard_map/ppermute | solution.py:355
  35.7 0.0 collective-permute-start.8
  35.7 5.1 %collective-permute-done.11.refs_0_ = bf16[256,512]{1,0:T(8,128)(2,1)S(1)} collective-permute-done((bf16[256,512]{1,0:T(8,128)(2,1)S(1)}, bf16[256,512]{1,0:T(8,128)(2,1)S(1)}, u32[]{:S(2)}, u32[]{:S(2)}) %collective-permute-start.11) | collective-permute-done | bytes 262176 | tf_op jit(solution)/shard_map/ppermute | solution.py:355
  40.8 1.6 %collective-permute-start.12 = (bf16[256,512]{1,0:T(8,128)(2,1)S(1)}, bf16[256,512]{1,0:T(8,128)(2,1)S(1)}, u32[]{:S(2)}, u32[]{:S(2)}) collective-permute-start(bf16[256,512]{1,0:T(8,128)(2,1)S(1)} %collective-permute-done.11.refs_0_), channel_id=1, source_target_pairs={{0,4},{1,5},{2,6},{3,7},{4,0},{5,1},{6,2},{7,3},{8,12},{9,13},{10,... | collective-permute-start | bytes 786440 | tf_op jit(solution)/shard_map/ppermute | solution.py:355
  42.4 0.0 collective-permute-done.4.refs_2_
  42.4 1.5 %collective-permute-start.5 = (bf16[256,512]{1,0:T(8,128)(2,1)S(1)}, bf16[256,512]{1,0:T(8,128)(2,1)S(1)}, u32[]{:S(2)}, u32[]{:S(2)}) collective-permute-start(bf16[256,512]{1,0:T(8,128)(2,1)S(1)} %collective-permute-done.4.refs_2_), channel_id=1, source_target_pairs={{0,2},{1,3},{2,0},{3,1},{4,6},{5,7},{6,4},{7,5},{8,10},{9,11},{10,... | collective-permute-start | bytes 786440 | tf_op jit(solution)/shard_map/ppermute | solution.py:355
  43.9 0.0 collective-permute-done.17.refs_1_
  43.9 0.0 collective-permute-start.9
  43.9 0.0 collective-permute-done.15.refs_2_
  43.9 0.5 collective-permute-start.16
  44.4 0.0 collective-permute-done.8.refs_1_
  44.4 0.1 collective-permute-start.14
  44.5 4.2 %collective-permute-done.12.refs_0_ = bf16[256,512]{1,0:T(8,128)(2,1)S(1)} collective-permute-done((bf16[256,512]{1,0:T(8,128)(2,1)S(1)}, bf16[256,512]{1,0:T(8,128)(2,1)S(1)}, u32[]{:S(2)}, u32[]{:S(2)}) %collective-permute-start.12) | collective-permute-done | bytes 262176 | tf_op jit(solution)/shard_map/ppermute | solution.py:355
  48.6 0.0 collective-permute-start.13
  48.6 1.3 %collective-permute-done.5.refs_0_ = bf16[256,512]{1,0:T(8,128)(2,1)S(1)} collective-permute-done((bf16[256,512]{1,0:T(8,128)(2,1)S(1)}, bf16[256,512]{1,0:T(8,128)(2,1)S(1)}, u32[]{:S(2)}, u32[]{:S(2)}) %collective-permute-start.5) | collective-permute-done | bytes 262176 | tf_op jit(solution)/shard_map/ppermute | solution.py:355
  49.9 0.0 collective-permute-start.6
  49.9 0.0 copy-done
  49.9 0.4 shard_map.111.refs_4_
  50.3 0.4 shard_map.117.refs_4_
  50.8 0.0 collective-permute-done.9.refs_3_
  50.8 0.7 %shard_map.112.refs_1_ = f32[256,512]{1,0:T(8,128)S(1)} custom-call(bf16[4096,512]{1,0:T(8,128)(2,1)S(1)} %copy-done, bf16[256,512]{1,0:T(8,128)(2,1)S(1)} %collective-permute-done.7.refs_0_, bf16[256,512]{1,0:T(8,128)(2,1)S(1)} %collective-permute-done.8.refs_1_, bf16[256,512]{1,0:T(8,128)(2,1)S(1)} %collective-permute-done.4.refs_2_, ...), custom_call_target="tpu_custom_call" | custom-call | tf_op jit(solution)/shard_map/pallas_call | solution.py:295
  51.5 0.3 shard_map.113.refs_1_
  51.8 0.0 collective-permute-done.16.refs_3_
  51.8 0.0 collective-permute-done.14.refs_1_
  51.8 0.7 %shard_map.118.refs_1_ = f32[256,512]{1,0:T(8,128)S(1)} custom-call(bf16[4096,512]{1,0:T(8,128)(2,1)S(1)} %copy-done, bf16[256,512]{1,0:T(8,128)(2,1)S(1)} %collective-permute-done.11.refs_0_, bf16[256,512]{1,0:T(8,128)(2,1)S(1)} %collective-permute-done.14.refs_1_, bf16[256,512]{1,0:T(8,128)(2,1)S(1)} %collective-permute-done.15.refs_2_, ...), custom_call_target="tpu_custom_call" | custom-call | tf_op jit(solution)/shard_map/pallas_call | solution.py:295
  52.6 0.3 shard_map.119.refs_1_
  52.9 0.0 collective-permute-done.13.refs_0_
  52.9 1.0 %shard_map.120.refs_2_ = bf16[512,512]{1,0:T(8,128)(2,1)} custom-call(bf16[4096,512]{1,0:T(8,128)(2,1)S(1)} %copy-done, bf16[256,512]{1,0:T(8,128)(2,1)S(1)} %collective-permute-done.13.refs_0_, f32[256,512]{1,0:T(8,128)S(1)} %shard_map.119.refs_1_), custom_call_target="tpu_custom_call" | custom-call | tf_op jit(solution)/shard_map/pallas_call | solution.py:319
  53.9 0.0 collective-permute-done.6.refs_0_
  53.9 1.0 %shard_map.121 = bf16[512,512]{1,0:T(8,128)(2,1)} custom-call(bf16[4096,512]{1,0:T(8,128)(2,1)S(1)} %copy-done, bf16[256,512]{1,0:T(8,128)(2,1)S(1)} %collective-permute-done.6.refs_0_, f32[256,512]{1,0:T(8,128)S(1)} %shard_map.113.refs_1_, bf16[512,512]{1,0:T(8,128)(2,1)} %shard_map.120.refs_2_), custom_call_target="tpu_custom_call", output_to_operand_aliasing={{}: (3, {})} | custom-call | tf_op jit(solution)/shard_map/pallas_call | solution.py:319
Async XLA Ops:
  3.9 13.0 %copy-start.1 = (bf16[4096,512]{1,0:T(8,128)(2,1)S(1)}, bf16[4096,512]{1,0:T(8,128)(2,1)}, u32[]{:S(2)}) copy-start(bf16[4096,512]{1,0:T(8,128)(2,1)} %weight.14) | copy-start | bytes 12582916
  5.3 9.5 %collective-permute-start = (bf16[256,256]{1,0:T(8,128)(2,1)S(1)}, bf16[256,256]{1,0:T(8,128)(2,1)S(1)}, u32[]{:S(2)}, u32[]{:S(2)}) collective-permute-start(bf16[256,256]{1,0:T(8,128)(2,1)S(1)} %get-tuple-element.24.refs_4_.refs_2_), channel_id=1, source_target_pairs={{0,8},{8,16},{16,24},{24,0},{1,9},{9,17},{17,25},{25,1},{2,10},{10... | collective-permute-start | bytes 393224 | tf_op jit(solution)/shard_map/ppermute | solution.py:350
  8.4 8.3 %collective-permute-start.2 = (bf16[256,256]{1,0:T(8,128)(2,1)S(1)}, bf16[256,256]{1,0:T(8,128)(2,1)S(1)}, u32[]{:S(2)}, u32[]{:S(2)}) collective-permute-start(bf16[256,256]{1,0:T(8,128)(2,1)S(1)} %get-tuple-element.25.refs_3_), channel_id=1, source_target_pairs={{0,8},{8,16},{16,24},{24,0},{1,9},{9,17},{17,25},{25,1},{2,10},{10... | collective-permute-start | bytes 393224 | tf_op jit(solution)/shard_map/ppermute | solution.py:350
  14.8 7.9 %collective-permute-start.1 = (bf16[256,256]{1,0:T(8,128)(2,1)S(1)}, bf16[256,256]{1,0:T(8,128)(2,1)S(1)}, u32[]{:S(2)}, u32[]{:S(2)}) collective-permute-start(bf16[256,256]{1,0:T(8,128)(2,1)S(1)} %collective-permute-done.refs_2_.refs_0_), channel_id=1, source_target_pairs={{0,8},{8,16},{16,24},{24,0},{1,9},{9,17},{17,25},{25,1},{2,10},{10... | collective-permute-start | bytes 393224 | tf_op jit(solution)/shard_map/ppermute | solution.py:350
  16.8 7.6 %collective-permute-start.3 = (bf16[256,256]{1,0:T(8,128)(2,1)S(1)}, bf16[256,256]{1,0:T(8,128)(2,1)S(1)}, u32[]{:S(2)}, u32[]{:S(2)}) collective-permute-start(bf16[256,256]{1,0:T(8,128)(2,1)S(1)} %collective-permute-done.2.refs_3_.refs_1_), channel_id=1, source_target_pairs={{0,8},{8,16},{16,24},{24,0},{1,9},{9,17},{17,25},{25,1},{2,10},{10... | collective-permute-start | bytes 393224 | tf_op jit(solution)/shard_map/ppermute | solution.py:350
  19.7 30.2 %copy-start = (bf16[4096,512]{1,0:T(8,128)(2,1)S(1)}, bf16[4096,512]{1,0:T(8,128)(2,1)}, u32[]{:S(2)}) copy-start(bf16[4096,512]{1,0:T(8,128)(2,1)} %weight.19) | copy-start | bytes 12582916
  26.4 4.4 %collective-permute-start.10 = (bf16[256,512]{1,0:T(8,128)(2,1)S(1)}, bf16[256,512]{1,0:T(8,128)(2,1)S(1)}, u32[]{:S(2)}, u32[]{:S(2)}) collective-permute-start(bf16[256,512]{1,0:T(8,128)(2,1)S(1)} %shard_map.110.refs_0_), channel_id=1, source_target_pairs={{0,1},{1,0},{2,3},{3,2},{4,5},{5,4},{6,7},{7,6},{8,9},{9,8},{10,11... | collective-permute-start | bytes 786440 | tf_op jit(solution)/shard_map/ppermute | solution.py:355
  26.5 9.2 %collective-permute-start.7 = (bf16[256,512]{1,0:T(8,128)(2,1)S(1)}, bf16[256,512]{1,0:T(8,128)(2,1)S(1)}, u32[]{:S(2)}, u32[]{:S(2)}) collective-permute-start(bf16[256,512]{1,0:T(8,128)(2,1)S(1)} %shard_map.110.refs_0_), channel_id=1, source_target_pairs={{0,2},{1,3},{2,0},{3,1},{4,6},{5,7},{6,4},{7,5},{8,10},{9,11},{10,... | collective-permute-start | bytes 786440 | tf_op jit(solution)/shard_map/ppermute | solution.py:355
  28.7 12.1 %collective-permute-start.11 = (bf16[256,512]{1,0:T(8,128)(2,1)S(1)}, bf16[256,512]{1,0:T(8,128)(2,1)S(1)}, u32[]{:S(2)}, u32[]{:S(2)}) collective-permute-start(bf16[256,512]{1,0:T(8,128)(2,1)S(1)} %shard_map.116.refs_0_), channel_id=1, source_target_pairs={{0,2},{1,3},{2,0},{3,1},{4,6},{5,7},{6,4},{7,5},{8,10},{9,11},{10,... | collective-permute-start | bytes 786440 | tf_op jit(solution)/shard_map/ppermute | solution.py:355
  29.3 13.1 %collective-permute-start.4 = (bf16[256,512]{1,0:T(8,128)(2,1)S(1)}, bf16[256,512]{1,0:T(8,128)(2,1)S(1)}, u32[]{:S(2)}, u32[]{:S(2)}) collective-permute-start(bf16[256,512]{1,0:T(8,128)(2,1)S(1)} %shard_map.110.refs_0_), channel_id=1, source_target_pairs={{0,4},{1,5},{2,6},{3,7},{4,0},{5,1},{6,2},{7,3},{8,12},{9,13},{10,... | collective-permute-start | bytes 786440 | tf_op jit(solution)/shard_map/ppermute | solution.py:355
  30.9 13.0 %collective-permute-start.17 = (bf16[256,512]{1,0:T(8,128)(2,1)S(1)}, bf16[256,512]{1,0:T(8,128)(2,1)S(1)}, u32[]{:S(2)}, u32[]{:S(2)}) collective-permute-start(bf16[256,512]{1,0:T(8,128)(2,1)S(1)} %shard_map.116.refs_0_), channel_id=1, source_target_pairs={{0,1},{1,0},{2,3},{3,2},{4,5},{5,4},{6,7},{7,6},{8,9},{9,8},{10,11... | collective-permute-start | bytes 786440 | tf_op jit(solution)/shard_map/ppermute | solution.py:355
  30.9 13.0 %collective-permute-start.15 = (bf16[256,512]{1,0:T(8,128)(2,1)S(1)}, bf16[256,512]{1,0:T(8,128)(2,1)S(1)}, u32[]{:S(2)}, u32[]{:S(2)}) collective-permute-start(bf16[256,512]{1,0:T(8,128)(2,1)S(1)} %shard_map.116.refs_0_), channel_id=1, source_target_pairs={{0,4},{1,5},{2,6},{3,7},{4,0},{5,1},{6,2},{7,3},{8,12},{9,13},{10,... | collective-permute-start | bytes 786440 | tf_op jit(solution)/shard_map/ppermute | solution.py:355
  35.7 8.6 %collective-permute-start.8 = (bf16[256,512]{1,0:T(8,128)(2,1)S(1)}, bf16[256,512]{1,0:T(8,128)(2,1)S(1)}, u32[]{:S(2)}, u32[]{:S(2)}) collective-permute-start(bf16[256,512]{1,0:T(8,128)(2,1)S(1)} %collective-permute-done.7.refs_0_), channel_id=1, source_target_pairs={{0,1},{1,0},{2,3},{3,2},{4,5},{5,4},{6,7},{7,6},{8,9},{9,8},{10,11... | collective-permute-start | bytes 786440 | tf_op jit(solution)/shard_map/ppermute | solution.py:355
  40.8 7.8 %collective-permute-start.12 = (bf16[256,512]{1,0:T(8,128)(2,1)S(1)}, bf16[256,512]{1,0:T(8,128)(2,1)S(1)}, u32[]{:S(2)}, u32[]{:S(2)}) collective-permute-start(bf16[256,512]{1,0:T(8,128)(2,1)S(1)} %collective-permute-done.11.refs_0_), channel_id=1, source_target_pairs={{0,4},{1,5},{2,6},{3,7},{4,0},{5,1},{6,2},{7,3},{8,12},{9,13},{10,... | collective-permute-start | bytes 786440 | tf_op jit(solution)/shard_map/ppermute | solution.py:355
  42.4 7.5 %collective-permute-start.5 = (bf16[256,512]{1,0:T(8,128)(2,1)S(1)}, bf16[256,512]{1,0:T(8,128)(2,1)S(1)}, u32[]{:S(2)}, u32[]{:S(2)}) collective-permute-start(bf16[256,512]{1,0:T(8,128)(2,1)S(1)} %collective-permute-done.4.refs_2_), channel_id=1, source_target_pairs={{0,2},{1,3},{2,0},{3,1},{4,6},{5,7},{6,4},{7,5},{8,10},{9,11},{10,... | collective-permute-start | bytes 786440 | tf_op jit(solution)/shard_map/ppermute | solution.py:355
  43.9 6.9 %collective-permute-start.9 = (bf16[256,512]{1,0:T(8,128)(2,1)S(1)}, bf16[256,512]{1,0:T(8,128)(2,1)S(1)}, u32[]{:S(2)}, u32[]{:S(2)}) collective-permute-start(bf16[256,512]{1,0:T(8,128)(2,1)S(1)} %collective-permute-done.4.refs_2_), channel_id=1, source_target_pairs={{0,1},{1,0},{2,3},{3,2},{4,5},{5,4},{6,7},{7,6},{8,9},{9,8},{10,11... | collective-permute-start | bytes 786440 | tf_op jit(solution)/shard_map/ppermute | solution.py:355
  43.9 7.9 %collective-permute-start.16 = (bf16[256,512]{1,0:T(8,128)(2,1)S(1)}, bf16[256,512]{1,0:T(8,128)(2,1)S(1)}, u32[]{:S(2)}, u32[]{:S(2)}) collective-permute-start(bf16[256,512]{1,0:T(8,128)(2,1)S(1)} %collective-permute-done.15.refs_2_), channel_id=1, source_target_pairs={{0,1},{1,0},{2,3},{3,2},{4,5},{5,4},{6,7},{7,6},{8,9},{9,8},{10,11... | collective-permute-start | bytes 786440 | tf_op jit(solution)/shard_map/ppermute | solution.py:355
  44.4 7.4 %collective-permute-start.14 = (bf16[256,512]{1,0:T(8,128)(2,1)S(1)}, bf16[256,512]{1,0:T(8,128)(2,1)S(1)}, u32[]{:S(2)}, u32[]{:S(2)}) collective-permute-start(bf16[256,512]{1,0:T(8,128)(2,1)S(1)} %collective-permute-done.11.refs_0_), channel_id=1, source_target_pairs={{0,1},{1,0},{2,3},{3,2},{4,5},{5,4},{6,7},{7,6},{8,9},{9,8},{10,11... | collective-permute-start | bytes 786440 | tf_op jit(solution)/shard_map/ppermute | solution.py:355
  48.6 4.3 %collective-permute-start.13 = (bf16[256,512]{1,0:T(8,128)(2,1)S(1)}, bf16[256,512]{1,0:T(8,128)(2,1)S(1)}, u32[]{:S(2)}, u32[]{:S(2)}) collective-permute-start(bf16[256,512]{1,0:T(8,128)(2,1)S(1)} %collective-permute-done.12.refs_0_), channel_id=1, source_target_pairs={{0,1},{1,0},{2,3},{3,2},{4,5},{5,4},{6,7},{7,6},{8,9},{9,8},{10,11... | collective-permute-start | bytes 786440 | tf_op jit(solution)/shard_map/ppermute | solution.py:355
  49.9 4.0 %collective-permute-start.6 = (bf16[256,512]{1,0:T(8,128)(2,1)S(1)}, bf16[256,512]{1,0:T(8,128)(2,1)S(1)}, u32[]{:S(2)}, u32[]{:S(2)}) collective-permute-start(bf16[256,512]{1,0:T(8,128)(2,1)S(1)} %collective-permute-done.5.refs_0_), channel_id=1, source_target_pairs={{0,1},{1,0},{2,3},{3,2},{4,5},{5,4},{6,7},{7,6},{8,9},{9,8},{10,11... | collective-permute-start | bytes 786440 | tf_op jit(solution)/shard_map/ppermute | solution.py:355

commit v2 on v1

--- a/solution.py
+++ b/solution.py
@@ -24,11 +24,14 @@
     return [pltpu.with_memory_space_constraint(a, pltpu.HBM) for a in arrays]
 
 
+STEP = 16
+
+
 def rotation_tables(block_rows, blocks):
     freqs = BASE ** (-2.0 * (np.arange(HEAD_DIM) % (HEAD_DIM // 2)) / HEAD_DIM)
-    row = np.arange(block_rows)[:, None] * freqs
-    start = (np.arange(blocks) * block_rows)[:, None] * freqs
-    tables = (np.cos(row), np.sin(row), np.cos(start), np.sin(start))
+    coarse = np.arange(0, block_rows * blocks, STEP)[:, None] * freqs
+    fine = np.arange(STEP)[:, None] * freqs
+    tables = (np.cos(coarse), np.sin(coarse), np.cos(fine), np.sin(fine))
     return [jnp.asarray(t, jnp.float32) for t in tables]
 
 
@@ -55,9 +58,9 @@
 
 
 def second_half_kernel(
-    tile, tokens, gain, key_weight, value_weight, row_cos, row_sin, start_cos, start_sin, segments,
+    tile, tokens, gain, key_weight, value_weight, coarse_cos, coarse_sin, fine_cos, fine_sin, segments,
     kv_ref, normed_ref, weight, first_tokens, gain_copy, cosine, sine, limits,
-    held, row_c, row_s, start_c, start_s, numbers, tile_sems, sems,
+    held, coarse_c, coarse_s, fine_c, fine_s, numbers, tile_sems, sems,
 ):
     rows, width = kv_ref.shape[0], key_weight.shape[1]
     steps = rows // tile
@@ -69,19 +72,21 @@
         )
         for i in range(steps)
     ]
+    groups = cosine.shape[0] // STEP
+    coarse = pl.ds(pl.multiple_of(lax.axis_index("seq") * groups, groups), groups)
     moves = [
         (gain, gain_copy),
         (key_weight, weight.at[:, :width]),
         (value_weight, weight.at[:, width:]),
-        (row_cos, row_c),
-        (row_sin, row_s),
-        (start_cos, start_c),
-        (start_sin, start_s),
+        (coarse_cos.at[coarse, :], coarse_c),
+        (coarse_sin.at[coarse, :], coarse_s),
+        (fine_cos, fine_c),
+        (fine_sin, fine_s),
         (tokens.at[:rows, :], first_tokens),
         (segments, numbers),
     ]
     moves = [pltpu.make_async_copy(a, b, sems.at[i]) for i, (a, b) in enumerate(moves)]
-    for move in [moves[8], moves[0]] + tiles + moves[1:8]:
+    for move in [moves[8], moves[0]] + tiles[:2] + moves[3:7] + tiles[2:] + moves[1:3] + moves[7:8]:
         move.start()
     moves[8].wait()
     for value in (1, 2):
@@ -95,13 +100,14 @@
         normed_ref[here, :] = normalise(held[here, :], gain_copy[...])
     for move in moves[3:7]:
         move.wait()
-    block = lax.axis_index("seq")
-    cos_b, sin_b = start_c[pl.ds(block, 1), :], start_s[pl.ds(block, 1), :]
-    cos_r, sin_r = row_c[...], row_s[...]
-    lane = lax.broadcasted_iota(jnp.int32, cos_r.shape, 1)
-    cosine[...] = cos_r * cos_b - sin_r * sin_b
-    turned = sin_r * cos_b + cos_r * sin_b
-    sine[...] = jnp.where(lane < HEAD_DIM // 2, -turned, turned)
+    cos_f, sin_f = fine_c[...], fine_s[...]
+    lane = lax.broadcasted_iota(jnp.int32, cos_f.shape, 1)
+    for group in range(groups):
+        cos_g, sin_g = coarse_c[group : group + 1, :], coarse_s[group : group + 1, :]
+        turned = sin_g * cos_f + cos_g * sin_f
+        here = slice(group * STEP, (group + 1) * STEP)
+        cosine[here, :] = cos_g * cos_f - sin_g * sin_f
+        sine[here, :] = jnp.where(lane < HEAD_DIM // 2, -turned, turned)
     moves[1].wait()
     moves[2].wait()
     key_value_of(normed_ref[...], weight[...], cosine[rows:, :], sine[rows:, :], kv_ref, slice(None))
@@ -111,7 +117,7 @@
 def second_half(tokens, gain, key_weight, value_weight, tables, segments):
     block_rows, depth = tokens.shape
     half, width = block_rows // 2, key_weight.shape[1]
-    tile = min(half, 64)
+    tile = min(half, 32)
     shape, bf16, f32 = jax.ShapeDtypeStruct, jnp.bfloat16, jnp.float32
     return pl.pallas_call(
         functools.partial(second_half_kernel, tile),
@@ -128,7 +134,8 @@
         in_specs=[HBM] * 9,
         out_specs=(VMEM,) * 8,
         scratch_shapes=[pltpu.VMEM((half, depth), bf16)]
-        + [pltpu.VMEM(t.shape, f32) for t in tables]
+        + [pltpu.VMEM((block_rows // STEP, HEAD_DIM), f32)] * 2
+        + [pltpu.VMEM((STEP, HEAD_DIM), f32)] * 2
         + [pltpu.VMEM(segments.shape, jnp.int32)]
         + [pltpu.SemaphoreType.DMA((half // tile,)), pltpu.SemaphoreType.DMA((9,))],
         compiler_params=PARAMS,
@@ -334,7 +341,12 @@
     total = block_rows * seq_count
     reach = min(WINDOW, total // 2)
     back = min((reach - 2) // half + 1, 2 * seq_count - 1)
-    ring = [(i, (i + 1) % seq_count) for i in range(seq_count)]
+
+    def onward(hop):
+        pairs = [(i, i + 1, 0) for i in range(hop - 1, seq_count - 1)]
+        pairs = pairs + [(seq_count - 1, hop - 1, 0)] + [(i, i, 1) for i in range(hop - 1)]
+        return [(a * tp_count + t, b * tp_count + (t ^ c)) for a, b, c in pairs for t in range(tp_count)]
+
 
     halves, normed, queries = [None] * (back + 2), [None, None], [None, None]
     halves[0], normed[1], weight, first_tokens, gain, cosine, sine, limits = second_half(
@@ -347,7 +359,7 @@
     )
     halves[1], normed[0] = first_half(first_tokens, gain, weight, cosine, sine)
     for distance in range(2, back + 2):
-        halves[distance] = lax.ppermute(halves[distance - 2], "seq", ring)
+        halves[distance] = lax.ppermute(halves[distance - 2], ("seq", "tp"), onward(distance // 2))
     for part in (1, 0):
         queries[part] = query(part, normed[part], query_weight, cosine, sine)
 

time: 55.3 us -> 52.4 us (0.948)
  waiting for transfers between devices: 24.7 us -> 21.8 us
    ppermute x4, waiting for transfers between devices: 9.82 us -> 7.61 us  [shards(): lax.ppermute(halves[distance - 2], ('seq', 'tp'), onward(distance // 2))]
    ppermute x14, waiting for transfers between devices: 14.9 us -> 14.2 us  [swap(): return lax.ppermute(x, 'tp', [(i, i ^ bit) for i in range(tp_count)])]
    ppermute x14, starting transfers between devices: 7.88 us -> 8.51 us  [swap(): return lax.ppermute(x, 'tp', [(i, i ^ bit) for i in range(tp_count)])]
  transfers between devices with their start and end apart: 18 -> 18, of which waited for: 8 -> 6; matrix products, arithmetic and copies ran while one was open for 0% -> 0% of each run, Pallas kernels for 16% -> 17%
where the time goes in v2:
time: 52.4 us; the launch traced here: 52.2 us
  waiting for transfers between devices  21.8 us (42%)
  Pallas kernels  16.9 us (32%)
  starting transfers between devices  13.2 us (25%)
    ppermute x14, waiting for transfers between devices, swap(): return lax.ppermute(x, 'tp', [(i, i ^ bit) for i in range(tp_count)])  14.2 us
    ppermute x14, starting transfers between devices, swap(): return lax.ppermute(x, 'tp', [(i, i ^ bit) for i in range(tp_count)])  8.51 us
    ppermute x4, waiting for transfers between devices, shards(): lax.ppermute(halves[distance - 2], ('seq', 'tp'), onward(distance // 2))  7.61 us
    ppermute x4, starting transfers between devices, shards(): lax.ppermute(halves[distance - 2], ('seq', 'tp'), onward(distance // 2))  4.69 us
    pallas_call x3, Pallas kernels, attend(): pl.pallas_call(functools.partial(attend_kernel, part, back, tuple(places)...  4.31 us
    pallas_call x1, Pallas kernels, second_half(): pl.pallas_call(functools.partial(second_half_kernel, tile), out_shape=(sh...  3.4 us
    pallas_call x6, Pallas kernels, product(): pl.pallas_call(functools.partial(product_kernel, bits, bool(extra)), out_...  2.91 us
    pallas_call x2, Pallas kernels, query(): pl.pallas_call(functools.partial(query_kernel, part), out_shape=jax.Shape...  2.76 us
  transfers between devices with their start and end apart: 18, of which 6 were waited for; matrix products, arithmetic and copies ran while one was open for 0% of the time, Pallas kernels for 17%

profile of v2, /device:TPU:0, one launch (start us, length us, event | category | flops | bytes accessed | tf_op | source)
XLA Modules:
  0.0 52.2 jit_solution(9822466584013201629)
XLA Ops:
  0.0 3.4 %second_half.1 = (bf16[256,256]{1,0:T(8,128)(2,1)S(1)}, bf16[256,4096]{1,0:T(8,128)(2,1)S(1)}, bf16[4096,256]{1,0:T(8,128)(2,1)S(1)}, bf16[256,4096]{1,0:T(8,128...) custom-call(bf16[512,4096]{1,0:T(8,128)(2,1)} %tokens.1, ...), custom_call_target="tpu_custom_call" | custom-call | tf_op jit(solution)/shard_map/second_half/pallas_call | solution.py:122
  3.4 0.0 copy-start.1
  3.4 1.4 %first_half.1 = (bf16[256,256]{1,0:T(8,128)(2,1)S(1)}, bf16[256,4096]{1,0:T(8,128)(2,1)S(1)}) custom-call(bf16[256,4096]{1,0:T(8,128)(2,1)S(1)} %get-tuple-element.18.tokens, f32[1,4096]{1,0:T(1,128)S(1)} %get-tuple-element.19.gain, bf16[4096,256]{1,0:T(8,128)(2,1)S(1)} %get-tuple-element.20.weight, f32[512,128]{1,0:T(8,128)S(1)} %get-tuple-element.21.cosine, ...), custom_call_target="tpu_custom_call" | custom-call | tf_op jit(solution)/shard_map/first_half/pallas_call | solution.py:154
  4.8 3.1 %collective-permute-start = (bf16[256,256]{1,0:T(8,128)(2,1)S(1)}, bf16[256,256]{1,0:T(8,128)(2,1)S(1)}, u32[]{:S(2)}, u32[]{:S(2)}) collective-permute-start(bf16[256,256]{1,0:T(8,128)(2,1)S(1)} %get-tuple-element.24.refs_4_.refs_2_), channel_id=1, source_target_pairs={{0,8},{1,9},{2,10},{3,11},{4,12},{5,13},{6,14},{7,15},{8,16},{9,17... | collective-permute-start | bytes 393224 | tf_op jit(solution)/shard_map/ppermute | solution.py:362
  7.9 1.6 %collective-permute-start.2 = (bf16[256,256]{1,0:T(8,128)(2,1)S(1)}, bf16[256,256]{1,0:T(8,128)(2,1)S(1)}, u32[]{:S(2)}, u32[]{:S(2)}) collective-permute-start(bf16[256,256]{1,0:T(8,128)(2,1)S(1)} %get-tuple-element.25.refs_3_), channel_id=1, source_target_pairs={{0,8},{1,9},{2,10},{3,11},{4,12},{5,13},{6,14},{7,15},{8,16},{9,17... | collective-permute-start | bytes 393224 | tf_op jit(solution)/shard_map/ppermute | solution.py:362
  9.5 4.8 %collective-permute-done.refs_2_.refs_0_ = bf16[256,256]{1,0:T(8,128)(2,1)S(1)} collective-permute-done((bf16[256,256]{1,0:T(8,128)(2,1)S(1)}, bf16[256,256]{1,0:T(8,128)(2,1)S(1)}, u32[]{:S(2)}, u32[]{:S(2)}) %collective-permute-start) | collective-permute-done | bytes 131104 | tf_op jit(solution)/shard_map/ppermute | solution.py:362
  14.3 0.0 collective-permute-start.1
  14.3 2.8 %collective-permute-done.2.refs_3_.refs_1_ = bf16[256,256]{1,0:T(8,128)(2,1)S(1)} collective-permute-done((bf16[256,256]{1,0:T(8,128)(2,1)S(1)}, bf16[256,256]{1,0:T(8,128)(2,1)S(1)}, u32[]{:S(2)}, u32[]{:S(2)}) %collective-permute-start.2) | collective-permute-done | bytes 131104 | tf_op jit(solution)/shard_map/ppermute | solution.py:362
  17.1 0.0 collective-permute-start.3
  17.1 0.0 copy-done.1
  17.1 1.4 %shard_map.109.q_ref = bf16[256,512]{1,0:T(8,128)(2,1)S(1)} custom-call(bf16[256,4096]{1,0:T(8,128)(2,1)S(1)} %get-tuple-element.23.normed, bf16[4096,512]{1,0:T(8,128)(2,1)S(1)} %copy-done.1, f32[512,128]{1,0:T(8,128)S(1)} %get-tuple-element.21.cosine, f32[512,128]{1,0:T(8,128)S(1)} %get-tuple-element.22.sine), custom_call_target="tpu_custom_call" | custom-call | tf_op jit(solution)/shard_map/pallas_call | solution.py:175
  18.5 1.4 %shard_map.114.q_ref = bf16[256,512]{1,0:T(8,128)(2,1)S(1)} custom-call(bf16[256,4096]{1,0:T(8,128)(2,1)S(1)} %get-tuple-element.26.normed, bf16[4096,512]{1,0:T(8,128)(2,1)S(1)} %copy-done.1, f32[512,128]{1,0:T(8,128)S(1)} %get-tuple-element.21.cosine, f32[512,128]{1,0:T(8,128)S(1)} %get-tuple-element.22.sine), custom_call_target="tpu_custom_call" | custom-call | tf_op jit(solution)/shard_map/pallas_call | solution.py:175
  19.9 0.0 copy-start
  19.9 1.6 %shard_map.115 = (f32[256,1024]{1,0:T(8,128)S(1)}, f32[256,512]{1,0:T(8,128)S(1)}) custom-call(s32[2,128]{1,0:T(2,128)S(1)} %get-tuple-element.17.limits, bf16[256,512]{1,0:T(8,128)(2,1)S(1)} %shard_map.114.q_ref, bf16[256,256]{1,0:T(8,128)(2,1)S(1)} %collective-permute-done.refs_2_.refs_0_, bf16[256,256]{1,0:T(8,128)(2,1)S(1)} %collective-permute-done.2.refs_3_.refs_1_, ...), custom_call_target="tpu_custom_call" | custom-call | tf_op jit(solution)/shard_map/pallas_call | solution.py:274
  21.6 0.0 collective-permute-done.1.refs_0_
  21.6 0.0 collective-permute-done.3.refs_1_.refs_0_
  21.6 2.0 %shard_map.110.refs_0_ = bf16[256,512]{1,0:T(8,128)(2,1)S(1)} custom-call(s32[2,128]{1,0:T(2,128)S(1)} %get-tuple-element.17.limits, bf16[256,512]{1,0:T(8,128)(2,1)S(1)} %shard_map.109.q_ref, bf16[256,256]{1,0:T(8,128)(2,1)S(1)} %collective-permute-done.1.refs_0_, bf16[256,256]{1,0:T(8,128)(2,1)S(1)} %collective-permute-done.3.refs_1_.refs_0_, ...), custom_call_target="tpu_custom_call" | custom-call | tf_op jit(solution)/shard_map/pallas_call | solution.py:274
  23.6 0.6 %collective-permute-start.10 = (bf16[256,512]{1,0:T(8,128)(2,1)S(1)}, bf16[256,512]{1,0:T(8,128)(2,1)S(1)}, u32[]{:S(2)}, u32[]{:S(2)}) collective-permute-start(bf16[256,512]{1,0:T(8,128)(2,1)S(1)} %shard_map.110.refs_0_), channel_id=1, source_target_pairs={{0,1},{1,0},{2,3},{3,2},{4,5},{5,4},{6,7},{7,6},{8,9},{9,8},{10,11... | collective-permute-start | bytes 786440 | tf_op jit(solution)/shard_map/ppermute | solution.py:367
  24.2 1.7 %collective-permute-start.7 = (bf16[256,512]{1,0:T(8,128)(2,1)S(1)}, bf16[256,512]{1,0:T(8,128)(2,1)S(1)}, u32[]{:S(2)}, u32[]{:S(2)}) collective-permute-start(bf16[256,512]{1,0:T(8,128)(2,1)S(1)} %shard_map.110.refs_0_), channel_id=1, source_target_pairs={{0,2},{1,3},{2,0},{3,1},{4,6},{5,7},{6,4},{7,5},{8,10},{9,11},{10,... | collective-permute-start | bytes 786440 | tf_op jit(solution)/shard_map/ppermute | solution.py:367
  25.9 0.6 %shard_map.116.refs_0_ = bf16[256,512]{1,0:T(8,128)(2,1)S(1)} custom-call(s32[2,128]{1,0:T(2,128)S(1)} %get-tuple-element.17.limits, bf16[256,512]{1,0:T(8,128)(2,1)S(1)} %shard_map.114.q_ref, bf16[256,256]{1,0:T(8,128)(2,1)S(1)} %collective-permute-done.3.refs_1_.refs_0_, f32[256,1024]{1,0:T(8,128)S(1)} %get-tuple-element.27.refs_1_, ...), custom_call_target="tpu_custom_call" | custom-call | tf_op jit(solution)/shard_map/pallas_call | solution.py:274
  26.6 0.4 collective-permute-start.11
  26.9 1.7 %collective-permute-start.4 = (bf16[256,512]{1,0:T(8,128)(2,1)S(1)}, bf16[256,512]{1,0:T(8,128)(2,1)S(1)}, u32[]{:S(2)}, u32[]{:S(2)}) collective-permute-start(bf16[256,512]{1,0:T(8,128)(2,1)S(1)} %shard_map.110.refs_0_), channel_id=1, source_target_pairs={{0,4},{1,5},{2,6},{3,7},{4,0},{5,1},{6,2},{7,3},{8,12},{9,13},{10,... | collective-permute-start | bytes 786440 | tf_op jit(solution)/shard_map/ppermute | solution.py:367
  28.7 0.0 collective-permute-start.17
  28.7 0.0 collective-permute-done.10.refs_1_
  28.7 0.3 collective-permute-start.15
  29.0 4.4 %collective-permute-done.7.refs_0_ = bf16[256,512]{1,0:T(8,128)(2,1)S(1)} collective-permute-done((bf16[256,512]{1,0:T(8,128)(2,1)S(1)}, bf16[256,512]{1,0:T(8,128)(2,1)S(1)}, u32[]{:S(2)}, u32[]{:S(2)}) %collective-permute-start.7) | collective-permute-done | bytes 262176 | tf_op jit(solution)/shard_map/ppermute | solution.py:367
  33.4 0.0 collective-permute-start.8
  33.4 4.7 %collective-permute-done.11.refs_0_ = bf16[256,512]{1,0:T(8,128)(2,1)S(1)} collective-permute-done((bf16[256,512]{1,0:T(8,128)(2,1)S(1)}, bf16[256,512]{1,0:T(8,128)(2,1)S(1)}, u32[]{:S(2)}, u32[]{:S(2)}) %collective-permute-start.11) | collective-permute-done | bytes 262176 | tf_op jit(solution)/shard_map/ppermute | solution.py:367
  38.1 1.7 %collective-permute-start.12 = (bf16[256,512]{1,0:T(8,128)(2,1)S(1)}, bf16[256,512]{1,0:T(8,128)(2,1)S(1)}, u32[]{:S(2)}, u32[]{:S(2)}) collective-permute-start(bf16[256,512]{1,0:T(8,128)(2,1)S(1)} %collective-permute-done.11.refs_0_), channel_id=1, source_target_pairs={{0,4},{1,5},{2,6},{3,7},{4,0},{5,1},{6,2},{7,3},{8,12},{9,13},{10,... | collective-permute-start | bytes 786440 | tf_op jit(solution)/shard_map/ppermute | solution.py:367
  39.9 0.0 collective-permute-done.4.refs_2_
  39.9 1.5 %collective-permute-start.5 = (bf16[256,512]{1,0:T(8,128)(2,1)S(1)}, bf16[256,512]{1,0:T(8,128)(2,1)S(1)}, u32[]{:S(2)}, u32[]{:S(2)}) collective-permute-start(bf16[256,512]{1,0:T(8,128)(2,1)S(1)} %collective-permute-done.4.refs_2_), channel_id=1, source_target_pairs={{0,2},{1,3},{2,0},{3,1},{4,6},{5,7},{6,4},{7,5},{8,10},{9,11},{10,... | collective-permute-start | bytes 786440 | tf_op jit(solution)/shard_map/ppermute | solution.py:367
  41.3 0.0 collective-permute-done.17.refs_1_
  41.3 0.0 collective-permute-start.9
  41.4 0.0 collective-permute-done.15.refs_2_
  41.4 0.5 collective-permute-start.16
  41.9 0.0 collective-permute-done.8.refs_1_
  41.9 0.1 collective-permute-start.14
  41.9 4.0 %collective-permute-done.12.refs_0_ = bf16[256,512]{1,0:T(8,128)(2,1)S(1)} collective-permute-done((bf16[256,512]{1,0:T(8,128)(2,1)S(1)}, bf16[256,512]{1,0:T(8,128)(2,1)S(1)}, u32[]{:S(2)}, u32[]{:S(2)}) %collective-permute-start.12) | collective-permute-done | bytes 262176 | tf_op jit(solution)/shard_map/ppermute | solution.py:367
  45.9 0.0 collective-permute-start.13
  46.0 1.1 %collective-permute-done.5.refs_0_ = bf16[256,512]{1,0:T(8,128)(2,1)S(1)} collective-permute-done((bf16[256,512]{1,0:T(8,128)(2,1)S(1)}, bf16[256,512]{1,0:T(8,128)(2,1)S(1)}, u32[]{:S(2)}, u32[]{:S(2)}) %collective-permute-start.5) | collective-permute-done | bytes 262176 | tf_op jit(solution)/shard_map/ppermute | solution.py:367
  47.0 0.0 collective-permute-start.6
  47.0 0.0 copy-done
  47.0 0.4 shard_map.111.refs_4_
  47.5 0.4 shard_map.117.refs_4_
  47.9 0.0 collective-permute-done.9.refs_3_
  47.9 0.7 %shard_map.112.refs_1_ = f32[256,512]{1,0:T(8,128)S(1)} custom-call(bf16[4096,512]{1,0:T(8,128)(2,1)S(1)} %copy-done, bf16[256,512]{1,0:T(8,128)(2,1)S(1)} %collective-permute-done.7.refs_0_, bf16[256,512]{1,0:T(8,128)(2,1)S(1)} %collective-permute-done.8.refs_1_, bf16[256,512]{1,0:T(8,128)(2,1)S(1)} %collective-permute-done.4.refs_2_, ...), custom_call_target="tpu_custom_call" | custom-call | tf_op jit(solution)/shard_map/pallas_call | solution.py:302
  48.6 0.3 shard_map.113.refs_1_
  48.9 0.0 collective-permute-done.16.refs_3_
  49.0 0.0 collective-permute-done.14.refs_1_
  49.0 0.7 %shard_map.118.refs_1_ = f32[256,512]{1,0:T(8,128)S(1)} custom-call(bf16[4096,512]{1,0:T(8,128)(2,1)S(1)} %copy-done, bf16[256,512]{1,0:T(8,128)(2,1)S(1)} %collective-permute-done.11.refs_0_, bf16[256,512]{1,0:T(8,128)(2,1)S(1)} %collective-permute-done.14.refs_1_, bf16[256,512]{1,0:T(8,128)(2,1)S(1)} %collective-permute-done.15.refs_2_, ...), custom_call_target="tpu_custom_call" | custom-call | tf_op jit(solution)/shard_map/pallas_call | solution.py:302
  49.7 0.3 shard_map.119.refs_1_
  50.0 0.0 collective-permute-done.13.refs_0_
  50.0 1.0 %shard_map.120.refs_2_ = bf16[512,512]{1,0:T(8,128)(2,1)} custom-call(bf16[4096,512]{1,0:T(8,128)(2,1)S(1)} %copy-done, bf16[256,512]{1,0:T(8,128)(2,1)S(1)} %collective-permute-done.13.refs_0_, f32[256,512]{1,0:T(8,128)S(1)} %shard_map.119.refs_1_), custom_call_target="tpu_custom_call" | custom-call | tf_op jit(solution)/shard_map/pallas_call | solution.py:326
  51.0 0.0 collective-permute-done.6.refs_0_
  51.1 1.0 %shard_map.121 = bf16[512,512]{1,0:T(8,128)(2,1)} custom-call(bf16[4096,512]{1,0:T(8,128)(2,1)S(1)} %copy-done, bf16[256,512]{1,0:T(8,128)(2,1)S(1)} %collective-permute-done.6.refs_0_, f32[256,512]{1,0:T(8,128)S(1)} %shard_map.113.refs_1_, bf16[512,512]{1,0:T(8,128)(2,1)} %shard_map.120.refs_2_), custom_call_target="tpu_custom_call", output_to_operand_aliasing={{}: (3, {})} | custom-call | tf_op jit(solution)/shard_map/pallas_call | solution.py:326
Async XLA Ops:
  3.4 13.7 %copy-start.1 = (bf16[4096,512]{1,0:T(8,128)(2,1)S(1)}, bf16[4096,512]{1,0:T(8,128)(2,1)}, u32[]{:S(2)}) copy-start(bf16[4096,512]{1,0:T(8,128)(2,1)} %weight.14) | copy-start | bytes 12582916
  4.8 9.5 %collective-permute-start = (bf16[256,256]{1,0:T(8,128)(2,1)S(1)}, bf16[256,256]{1,0:T(8,128)(2,1)S(1)}, u32[]{:S(2)}, u32[]{:S(2)}) collective-permute-start(bf16[256,256]{1,0:T(8,128)(2,1)S(1)} %get-tuple-element.24.refs_4_.refs_2_), channel_id=1, source_target_pairs={{0,8},{1,9},{2,10},{3,11},{4,12},{5,13},{6,14},{7,15},{8,16},{9,17... | collective-permute-start | bytes 393224 | tf_op jit(solution)/shard_map/ppermute | solution.py:362
  7.9 9.2 %collective-permute-start.2 = (bf16[256,256]{1,0:T(8,128)(2,1)S(1)}, bf16[256,256]{1,0:T(8,128)(2,1)S(1)}, u32[]{:S(2)}, u32[]{:S(2)}) collective-permute-start(bf16[256,256]{1,0:T(8,128)(2,1)S(1)} %get-tuple-element.25.refs_3_), channel_id=1, source_target_pairs={{0,8},{1,9},{2,10},{3,11},{4,12},{5,13},{6,14},{7,15},{8,16},{9,17... | collective-permute-start | bytes 393224 | tf_op jit(solution)/shard_map/ppermute | solution.py:362
  14.3 7.3 %collective-permute-start.1 = (bf16[256,256]{1,0:T(8,128)(2,1)S(1)}, bf16[256,256]{1,0:T(8,128)(2,1)S(1)}, u32[]{:S(2)}, u32[]{:S(2)}) collective-permute-start(bf16[256,256]{1,0:T(8,128)(2,1)S(1)} %collective-permute-done.refs_2_.refs_0_), channel_id=1, source_target_pairs={{8,16},{9,17},{10,18},{11,19},{12,20},{13,21},{14,22},{15,23},{16,... | collective-permute-start | bytes 393224 | tf_op jit(solution)/shard_map/ppermute | solution.py:362
  17.1 4.5 %collective-permute-start.3 = (bf16[256,256]{1,0:T(8,128)(2,1)S(1)}, bf16[256,256]{1,0:T(8,128)(2,1)S(1)}, u32[]{:S(2)}, u32[]{:S(2)}) collective-permute-start(bf16[256,256]{1,0:T(8,128)(2,1)S(1)} %collective-permute-done.2.refs_3_.refs_1_), channel_id=1, source_target_pairs={{8,16},{9,17},{10,18},{11,19},{12,20},{13,21},{14,22},{15,23},{16,... | collective-permute-start | bytes 393224 | tf_op jit(solution)/shard_map/ppermute | solution.py:362
  19.9 27.1 %copy-start = (bf16[4096,512]{1,0:T(8,128)(2,1)S(1)}, bf16[4096,512]{1,0:T(8,128)(2,1)}, u32[]{:S(2)}) copy-start(bf16[4096,512]{1,0:T(8,128)(2,1)} %weight.19) | copy-start | bytes 12582916
  23.6 5.1 %collective-permute-start.10 = (bf16[256,512]{1,0:T(8,128)(2,1)S(1)}, bf16[256,512]{1,0:T(8,128)(2,1)S(1)}, u32[]{:S(2)}, u32[]{:S(2)}) collective-permute-start(bf16[256,512]{1,0:T(8,128)(2,1)S(1)} %shard_map.110.refs_0_), channel_id=1, source_target_pairs={{0,1},{1,0},{2,3},{3,2},{4,5},{5,4},{6,7},{7,6},{8,9},{9,8},{10,11... | collective-permute-start | bytes 786440 | tf_op jit(solution)/shard_map/ppermute | solution.py:367
  24.2 9.2 %collective-permute-start.7 = (bf16[256,512]{1,0:T(8,128)(2,1)S(1)}, bf16[256,512]{1,0:T(8,128)(2,1)S(1)}, u32[]{:S(2)}, u32[]{:S(2)}) collective-permute-start(bf16[256,512]{1,0:T(8,128)(2,1)S(1)} %shard_map.110.refs_0_), channel_id=1, source_target_pairs={{0,2},{1,3},{2,0},{3,1},{4,6},{5,7},{6,4},{7,5},{8,10},{9,11},{10,... | collective-permute-start | bytes 786440 | tf_op jit(solution)/shard_map/ppermute | solution.py:367
  26.6 11.6 %collective-permute-start.11 = (bf16[256,512]{1,0:T(8,128)(2,1)S(1)}, bf16[256,512]{1,0:T(8,128)(2,1)S(1)}, u32[]{:S(2)}, u32[]{:S(2)}) collective-permute-start(bf16[256,512]{1,0:T(8,128)(2,1)S(1)} %shard_map.116.refs_0_), channel_id=1, source_target_pairs={{0,2},{1,3},{2,0},{3,1},{4,6},{5,7},{6,4},{7,5},{8,10},{9,11},{10,... | collective-permute-start | bytes 786440 | tf_op jit(solution)/shard_map/ppermute | solution.py:367
  26.9 12.9 %collective-permute-start.4 = (bf16[256,512]{1,0:T(8,128)(2,1)S(1)}, bf16[256,512]{1,0:T(8,128)(2,1)S(1)}, u32[]{:S(2)}, u32[]{:S(2)}) collective-permute-start(bf16[256,512]{1,0:T(8,128)(2,1)S(1)} %shard_map.110.refs_0_), channel_id=1, source_target_pairs={{0,4},{1,5},{2,6},{3,7},{4,0},{5,1},{6,2},{7,3},{8,12},{9,13},{10,... | collective-permute-start | bytes 786440 | tf_op jit(solution)/shard_map/ppermute | solution.py:367
  28.7 12.7 %collective-permute-start.17 = (bf16[256,512]{1,0:T(8,128)(2,1)S(1)}, bf16[256,512]{1,0:T(8,128)(2,1)S(1)}, u32[]{:S(2)}, u32[]{:S(2)}) collective-permute-start(bf16[256,512]{1,0:T(8,128)(2,1)S(1)} %shard_map.116.refs_0_), channel_id=1, source_target_pairs={{0,1},{1,0},{2,3},{3,2},{4,5},{5,4},{6,7},{7,6},{8,9},{9,8},{10,11... | collective-permute-start | bytes 786440 | tf_op jit(solution)/shard_map/ppermute | solution.py:367
  28.7 12.7 %collective-permute-start.15 = (bf16[256,512]{1,0:T(8,128)(2,1)S(1)}, bf16[256,512]{1,0:T(8,128)(2,1)S(1)}, u32[]{:S(2)}, u32[]{:S(2)}) collective-permute-start(bf16[256,512]{1,0:T(8,128)(2,1)S(1)} %shard_map.116.refs_0_), channel_id=1, source_target_pairs={{0,4},{1,5},{2,6},{3,7},{4,0},{5,1},{6,2},{7,3},{8,12},{9,13},{10,... | collective-permute-start | bytes 786440 | tf_op jit(solution)/shard_map/ppermute | solution.py:367
  33.4 8.5 %collective-permute-start.8 = (bf16[256,512]{1,0:T(8,128)(2,1)S(1)}, bf16[256,512]{1,0:T(8,128)(2,1)S(1)}, u32[]{:S(2)}, u32[]{:S(2)}) collective-permute-start(bf16[256,512]{1,0:T(8,128)(2,1)S(1)} %collective-permute-done.7.refs_0_), channel_id=1, source_target_pairs={{0,1},{1,0},{2,3},{3,2},{4,5},{5,4},{6,7},{7,6},{8,9},{9,8},{10,11... | collective-permute-start | bytes 786440 | tf_op jit(solution)/shard_map/ppermute | solution.py:367
  38.1 7.8 %collective-permute-start.12 = (bf16[256,512]{1,0:T(8,128)(2,1)S(1)}, bf16[256,512]{1,0:T(8,128)(2,1)S(1)}, u32[]{:S(2)}, u32[]{:S(2)}) collective-permute-start(bf16[256,512]{1,0:T(8,128)(2,1)S(1)} %collective-permute-done.11.refs_0_), channel_id=1, source_target_pairs={{0,4},{1,5},{2,6},{3,7},{4,0},{5,1},{6,2},{7,3},{8,12},{9,13},{10,... | collective-permute-start | bytes 786440 | tf_op jit(solution)/shard_map/ppermute | solution.py:367
  39.9 7.2 %collective-permute-start.5 = (bf16[256,512]{1,0:T(8,128)(2,1)S(1)}, bf16[256,512]{1,0:T(8,128)(2,1)S(1)}, u32[]{:S(2)}, u32[]{:S(2)}) collective-permute-start(bf16[256,512]{1,0:T(8,128)(2,1)S(1)} %collective-permute-done.4.refs_2_), channel_id=1, source_target_pairs={{0,2},{1,3},{2,0},{3,1},{4,6},{5,7},{6,4},{7,5},{8,10},{9,11},{10,... | collective-permute-start | bytes 786440 | tf_op jit(solution)/shard_map/ppermute | solution.py:367
  41.3 6.6 %collective-permute-start.9 = (bf16[256,512]{1,0:T(8,128)(2,1)S(1)}, bf16[256,512]{1,0:T(8,128)(2,1)S(1)}, u32[]{:S(2)}, u32[]{:S(2)}) collective-permute-start(bf16[256,512]{1,0:T(8,128)(2,1)S(1)} %collective-permute-done.4.refs_2_), channel_id=1, source_target_pairs={{0,1},{1,0},{2,3},{3,2},{4,5},{5,4},{6,7},{7,6},{8,9},{9,8},{10,11... | collective-permute-start | bytes 786440 | tf_op jit(solution)/shard_map/ppermute | solution.py:367
  41.4 7.6 %collective-permute-start.16 = (bf16[256,512]{1,0:T(8,128)(2,1)S(1)}, bf16[256,512]{1,0:T(8,128)(2,1)S(1)}, u32[]{:S(2)}, u32[]{:S(2)}) collective-permute-start(bf16[256,512]{1,0:T(8,128)(2,1)S(1)} %collective-permute-done.15.refs_2_), channel_id=1, source_target_pairs={{0,1},{1,0},{2,3},{3,2},{4,5},{5,4},{6,7},{7,6},{8,9},{9,8},{10,11... | collective-permute-start | bytes 786440 | tf_op jit(solution)/shard_map/ppermute | solution.py:367
  41.9 7.1 %collective-permute-start.14 = (bf16[256,512]{1,0:T(8,128)(2,1)S(1)}, bf16[256,512]{1,0:T(8,128)(2,1)S(1)}, u32[]{:S(2)}, u32[]{:S(2)}) collective-permute-start(bf16[256,512]{1,0:T(8,128)(2,1)S(1)} %collective-permute-done.11.refs_0_), channel_id=1, source_target_pairs={{0,1},{1,0},{2,3},{3,2},{4,5},{5,4},{6,7},{7,6},{8,9},{9,8},{10,11... | collective-permute-start | bytes 786440 | tf_op jit(solution)/shard_map/ppermute | solution.py:367
  45.9 4.1 %collective-permute-start.13 = (bf16[256,512]{1,0:T(8,128)(2,1)S(1)}, bf16[256,512]{1,0:T(8,128)(2,1)S(1)}, u32[]{:S(2)}, u32[]{:S(2)}) collective-permute-start(bf16[256,512]{1,0:T(8,128)(2,1)S(1)} %collective-permute-done.12.refs_0_), channel_id=1, source_target_pairs={{0,1},{1,0},{2,3},{3,2},{4,5},{5,4},{6,7},{7,6},{8,9},{9,8},{10,11... | collective-permute-start | bytes 786440 | tf_op jit(solution)/shard_map/ppermute | solution.py:367
  47.0 4.0 %collective-permute-start.6 = (bf16[256,512]{1,0:T(8,128)(2,1)S(1)}, bf16[256,512]{1,0:T(8,128)(2,1)S(1)}, u32[]{:S(2)}, u32[]{:S(2)}) collective-permute-start(bf16[256,512]{1,0:T(8,128)(2,1)S(1)} %collective-permute-done.5.refs_0_), channel_id=1, source_target_pairs={{0,1},{1,0},{2,3},{3,2},{4,5},{5,4},{6,7},{7,6},{8,9},{9,8},{10,11... | collective-permute-start | bytes 786440 | tf_op jit(solution)/shard_map/ppermute | solution.py:367
